TPU v7x, 512 devices: a whole 4x8x8 slice. The times are simulated.
512 devices in a mesh: dom: 64 (over x, y, core), mem: 8 (over z).
Axes of the slice: x: 4, y: 8, z: 8, core: 2. Of those that a mesh axis runs over, the one named last changes fastest.
Arguments:
- ensemble: bfloat16 [48, 32, 262144], P('mem', None, 'dom'), may hold values from -6 to 6
- observed: float32 [32, 65536], P(None, 'dom'), may hold values from -6 to 6
- tile_weight: bfloat16 [6144, 128, 128], P('dom')
- tile_block: int32 [6144], P('dom'), may hold values from 0 to 31
- tile_target: int32 [6144], P('dom'), may hold values from 0 to 511, as said below
- tile_count: int32 [64], P('dom'), may hold values from 48 to 96, as said below
Outputs:
- crps: float32 [32, 65536], P(None, 'dom')
Inputs may be any that keep to these rules, and one draw needn't show every extreme that they name: `tile_block`: a slot's source block, counted within its partition's cells. `tile_target`: slot k belongs to partition p = k // 96; its target tile is owned by one of the partitions p - 4 to p + 4, where partition o owns the 8 target tiles from o * 8 on. The live slots of partition p are the first tile_count[p] of its list; the rest are padding.
All inputs are finite; a program needn't handle non-finite values.
Results may differ from a plain program's by a relative error of at most 0.0003.
Values sent between devices are 32-bit elements; how exact they have to be, the bound alone decides.
No kernel may reach another device: no remote copies, remote signals or barrier semaphores. Data moves between devices by JAX's collectives and lax.ppermute only.
A program may use at most 64 MiB of HBM per device.

v0:
```python
import functools

import jax
import jax.numpy as jnp
from jax import lax
from jax.experimental import pallas as pl
from jax.experimental.pallas import tpu as pltpu
from jax.sharding import PartitionSpec as P


CHUNKS = (16, 16)

FAR = {4: 0, -3: 1, -4: 2}
NEAR = {2: 0, 3: 1, 0: 2, -1: 3, -2: 4, 1: 5}
UNROLL = 4


def coded(table):
    return sum(table.get(u, 7) << (3 * (u + 4)) for u in range(-4, 5))


def remap_kernel(codes, parts, split, chunks, block_hbm, target_hbm, count_hbm, ens_hbm, weight_hbm, *rest):
    outs, (acc, ens, weights, blocks, targets, count, slots, sems) = rest[:-8], rest[-8:]
    groups, levels, _ = ens.shape
    total = targets.shape[0]
    owned = 8
    small = [
        pltpu.make_async_copy(source, target, sems.at[index])
        for index, (source, target) in enumerate(((target_hbm, targets), (count_hbm, count), (block_hbm, blocks)))
    ]
    large = [pltpu.make_async_copy(ens_hbm.at[group], ens.at[group], sems.at[3 + group]) for group in range(groups)]
    pieces = 4
    span = total // pieces
    for piece in range(pieces):
        part = pl.ds(piece * span, span)
        large.append(pltpu.make_async_copy(weight_hbm.at[part], weights.at[part], sems.at[3 + groups + piece]))
    for copy in small + large:
        copy.start()
    device = lax.axis_index("dom")
    side = 1 - 2 * lax.rem(device, 2)
    dump = parts * owned

    def cleared(tile, carry):
        acc[tile] = jnp.zeros(acc.shape[1:], jnp.float32)
        return carry

    lax.fori_loop(0, dump, cleared, 0)
    for copy in small:
        copy.wait()
    live = count[0]

    def listed(slot, found):
        target = targets[slot]
        u = side * ((target >> 3) - device)
        code = (codes >> (3 * (u + 4))) & 7
        slots[found] = slot * 256 + code * owned + (target & 7)
        return found + jnp.where((code < 7) & (slot < live), 1, 0)

    found = lax.fori_loop(0, total, listed, jnp.int32(0), unroll=8)
    for extra in range(UNROLL):
        slots[found + extra] = dump
    for copy in large:
        copy.wait()

    def added(step, carry):
        results = []
        for offset in range(UNROLL):
            entry = slots[step * UNROLL + offset]
            slot = entry >> 8
            first = pl.multiple_of(blocks[slot] * 128, 128)
            picked = ens[:, :, pl.ds(first, 128)].reshape(groups * levels, 128)
            results.append(
                (entry & 255, jnp.dot(picked, weights[slot], preferred_element_type=jnp.float32))
            )
        for tile, result in results:
            acc[tile] += result
        return carry

    lax.fori_loop(0, (found + UNROLL - 1) // UNROLL, added, 0)

    def stored(tile, carry):
        start = 0
        for index, length in enumerate(chunks):
            for low, high, out in ((0, split, outs[2 * index]), (split, parts, outs[2 * index + 1])):
                for part in range(low, high):
                    for group in range(groups):
                        out[part - low, tile, group] = acc[part * owned + tile, pl.ds(group * levels + start, length)]
            start += length
        return carry

    lax.fori_loop(0, owned, stored, 0)


def remap(table, parts, split, chunks, limit, ensemble, tile_weight, tile_block, tile_target, tile_count):
    groups, levels, _ = ensemble.shape
    slots = tile_block.shape[0]
    shapes = []
    for length in chunks:
        for count in (split, parts - split):
            shapes.append(jax.ShapeDtypeStruct((count, 8, groups, length, 128), jnp.float32))
    outs = pl.pallas_call(
        functools.partial(remap_kernel, coded(table), parts, split, chunks),
        out_shape=shapes,
        in_specs=[pl.BlockSpec(memory_space=pltpu.HBM)] * 5,
        out_specs=[pl.BlockSpec(memory_space=pltpu.VMEM)] * len(shapes),
        scratch_shapes=[
            pltpu.VMEM((parts * 8 + 1, groups * levels, 128), jnp.float32),
            pltpu.VMEM(ensemble.shape, ensemble.dtype),
            pltpu.VMEM(tile_weight.shape, tile_weight.dtype),
            pltpu.SMEM((slots,), jnp.int32),
            pltpu.SMEM((slots,), jnp.int32),
            pltpu.SMEM((1,), jnp.int32),
            pltpu.SMEM((slots + UNROLL,), jnp.int32),
            pltpu.SemaphoreType.DMA((3 + groups + 4,)),
        ],
        cost_estimate=pl.CostEstimate(
            flops=2 * slots * groups * levels * 128 * 128, bytes_accessed=12_000_000, transcendentals=0
        ),
        compiler_params=pltpu.CompilerParams(vmem_limit_bytes=limit * 1024 * 1024),
    )(tile_block, tile_target, tile_count, ensemble, tile_weight)
    return [outs[2 * index : 2 * index + 2] for index in range(len(chunks))]


def score_kernel(first, copies, members_ref, observed_ref, *rest):
    before, out = rest[:-1], rest[-1]
    members, length, cells = members_ref.shape
    column = pl.multiple_of(lax.axis_index("mem") * cells, cells)
    done = 0
    scores = []
    for ref in before:
        scores.append((done, ref[...]))
        done += ref.shape[0]
    for low in range(0, length, 8):
        observed = observed_ref[pl.ds(first + low, 8), pl.ds(column, cells)]
        skill = jnp.zeros((8, cells), jnp.float32)
        spread = jnp.zeros((8, cells), jnp.float32)
        values = [members_ref[member, pl.ds(low, 8)] for member in range(members)]
        for left in range(members):
            skill = skill + jnp.abs(values[left] - observed)
            row = None
            for right in range(left + 1, members):
                gap = jnp.abs(values[left] - values[right])
                row = gap if row is None else row + gap
            if row is not None:
                spread = spread + row
        scores.append((done + low, skill / members - spread / (members * (members - 1.0))))
    if copies:
        for start, score in scores:
            for copy in range(copies):
                out[copy, start : start + score.shape[0]] = score
    else:
        for start, score in scores:
            out[start : start + score.shape[0]] = score


def scored(first, members, observed, before=(), copies=0):
    count, length, cells = members.shape
    done = sum(score.shape[0] for score in before)
    shape = (done + length, cells)
    if copies:
        shape = (copies, *shape)
    vmem = pl.BlockSpec(memory_space=pltpu.VMEM)
    return pl.pallas_call(
        functools.partial(score_kernel, first, copies),
        out_shape=jax.ShapeDtypeStruct(shape, jnp.float32),
        in_specs=[vmem] * (2 + len(before)),
        out_specs=vmem,
        cost_estimate=pl.CostEstimate(
            flops=3 * count * count * length * cells // 2, bytes_accessed=4 * count * length * cells, transcendentals=0
        ),
        compiler_params=pltpu.CompilerParams(vmem_limit_bytes=16 * 1024 * 1024),
    )(members, observed, *before)


def swapped(value):
    count = lax.axis_size("dom")
    return lax.ppermute(value, "dom", [(source, source ^ 1) for source in range(count)])


def passed_on(value, cross):
    count = lax.axis_size("dom")
    pairs = []
    for source in range(count):
        side = 1 - 2 * (source % 2)
        target = source + side * (3 if cross else 2)
        if 0 <= target < count:
            pairs.append((source, target))
    return lax.ppermute(value, "dom", pairs)


def on_device(ensemble, observed, tile_weight, tile_block, tile_target, tile_count):
    groups, levels, _ = ensemble.shape
    tiles = (ensemble, tile_weight, tile_block, tile_target, tile_count)
    far = remap(FAR, 3, 1, CHUNKS, 61, *tiles)
    ahead = []
    for keep, give in far:
        from_core = swapped(give)
        message = lax.dynamic_update_slice_in_dim(from_core, from_core[:1] + keep, 0, 0)
        ahead.append(passed_on(message, False))
    ((keep, give),) = remap(NEAR, 6, 3, (levels,), 18, *tiles)
    from_core = swapped(give)
    hops = []
    first = 0
    before = None
    for index, length in enumerate(CHUNKS):
        part = slice(first, first + length)
        farther = ahead[index]
        if index:
            farther, before = lax.optimization_barrier((farther, before))
        same = keep[0, :, :, part] + from_core[0, :, :, part] + farther[0]
        cross = keep[1, :, :, part] + from_core[1, :, :, part] + farther[1]
        before = same
        same = passed_on(same, False)
        cross = passed_on(cross, True)
        hops.append((same, cross))
        first += length
    scores = []
    first = 0
    for index, length in enumerate(CHUNKS):
        part = slice(first, first + length)
        arrived = hops[index]
        if index:
            arrived, before = lax.optimization_barrier((arrived, summed))
        summed = keep[2, :, :, part] + from_core[2, :, :, part] + arrived[0] + arrived[1]
        regrouped = lax.all_to_all(summed, "mem", split_axis=0, concat_axis=0, tiled=True)
        regrouped = regrouped.reshape(8 * groups, length, 128)
        if index + 1 < len(CHUNKS):
            scores.append(scored(first, regrouped, observed))
        else:
            copies = scored(first, regrouped, observed, scores, lax.axis_size("mem"))
        first += length
    pieces = lax.all_to_all(copies, "mem", split_axis=0, concat_axis=0, tiled=True)
    return jnp.moveaxis(pieces, 0, 1).reshape(observed.shape)


def solution(mesh):
    return jax.shard_map(
        on_device,
        mesh=mesh,
        in_specs=(
            P("mem", None, "dom"),
            P(None, "dom"),
            P("dom", None, None),
            P("dom"),
            P("dom"),
            P("dom"),
        ),
        out_specs=P(None, "dom"),
        check_vma=False,
    )
```

profile of v0, /device:TPU:18, one launch (start us, length us, event | category | flops | bytes accessed | tf_op | source)
XLA Modules:
  0.0 120.8 jit_solution(10631481540670064183)
XLA Ops:
  0.7 1.9 %copy-done = bf16[96,128,128]{2,1,0:T(8,128)(2,1)S(1)} copy-done((bf16[96,128,128]{2,1,0:T(8,128)(2,1)S(1)}, bf16[96,128,128]{2,1,0:T(8,128)(2,1)}, u32[]{:S(2)}) %copy-start) | copy-done | bytes 3145752
  5.3 6.2 %shard_map.64 = (f32[3,8,6,32,128]{4,3,2,1,0:T(8,128)S(1)}, f32[3,8,6,32,128]{4,3,2,1,0:T(8,128)}) custom-call(s32[96]{0:T(128)S(1)} %copy-done.3, s32[96]{0:T(128)S(1)} %copy-done.4, s32[1]{0:T(128)S(6)} %copy.12.count_hbm, bf16[6,32,4096]{2,1,0:T(8,128)(2,1)S(1)} %copy-done.1, bf16[96,128,128]{2,1,0:T(8,128)(2,1)S(1)} %copy-done), custom_call_target="tpu_custom_call" | custom-call | flops 603979776 | bytes 12000000 | tf_op jit(solution)/shard_map/pallas_call | solution.py:101
  11.5 1.9 %collective-permute-start = (f32[3,8,6,32,128]{4,3,2,1,0:T(8,128)}, f32[3,8,6,32,128]{4,3,2,1,0:T(8,128)}, u32[]{:S(2)}, u32[]{:S(2)}) collective-permute-start(f32[3,8,6,32,128]{4,3,2,1,0:T(8,128)} %get-tuple-element.15), channel_id=1, source_target_pairs={{0,8},{8,0},{16,24},{24,16},{32,40},{40,32},{48,56},{56,48},{64,72... | collective-permute-start | bytes 7077896 | tf_op jit(solution)/shard_map/ppermute | solution.py:177
  13.4 6.2 %shard_map.65 = (f32[1,8,6,16,128]{4,3,2,1,0:T(8,128)}, f32[2,8,6,16,128]{4,3,2,1,0:T(8,128)}, f32[1,8,6,16,128]{4,3,2,1,0:T(8,128)}, f32[2,8,6,16,128]{4,3,2,1,0:T(8,128)}) custom-call(s32[96]{0:T(128)} %block_hbm.3, s32[96]{0:T(128)} %target_hbm.3, s32[1]{0:T(128)S(6)} %copy.12.count_hbm, bf16[6,32,4096]{2,1,0:T(8,128)(2,1)} %ens_hbm.3, ...), custom_call_target="tpu_custom_call" | custom-call | flops 603979776 | bytes 12000000 | tf_op jit(solution)/shard_map/pallas_call | solution.py:101
  19.6 2.0 %collective-permute-start.3 = (f32[2,8,6,16,128]{4,3,2,1,0:T(8,128)}, f32[2,8,6,16,128]{4,3,2,1,0:T(8,128)S(1)}, u32[]{:S(2)}, u32[]{:S(2)}) collective-permute-start(f32[2,8,6,16,128]{4,3,2,1,0:T(8,128)} %get-tuple-element.18), channel_id=1, source_target_pairs={{0,8},{8,0},{16,24},{24,16},{32,40},{40,32},{48,56},{56,48},{64,72... | collective-permute-start | bytes 2359304 | tf_op jit(solution)/shard_map/ppermute | solution.py:177
  21.6 2.3 %collective-permute-start.1 = (f32[2,8,6,16,128]{4,3,2,1,0:T(8,128)}, f32[2,8,6,16,128]{4,3,2,1,0:T(8,128)S(1)}, u32[]{:S(2)}, u32[]{:S(2)}) collective-permute-start(f32[2,8,6,16,128]{4,3,2,1,0:T(8,128)} %get-tuple-element.16), channel_id=1, source_target_pairs={{0,8},{8,0},{16,24},{24,16},{32,40},{40,32},{48,56},{56,48},{64,72... | collective-permute-start | bytes 2359304 | tf_op jit(solution)/shard_map/ppermute | solution.py:177
  25.1 2.9 %collective-permute-start.4 = (f32[2,8,6,16,128]{4,3,2,1,0:T(8,128)S(1)}, f32[2,8,6,16,128]{4,3,2,1,0:T(8,128)S(1)}, u32[]{:S(2)}, u32[]{:S(2)}) collective-permute-start(f32[2,8,6,16,128]{4,3,2,1,0:T(8,128)S(1)} %fusion.7), channel_id=1, source_target_pairs={{0,16},{16,32},{24,8},{32,48},{40,24},{48,64},{56,40},{64,80},{72,... | collective-permute-start | bytes 2359304 | tf_op jit(solution)/shard_map/ppermute | solution.py:188
  29.1 4.9 %collective-permute-start.2 = (f32[2,8,6,16,128]{4,3,2,1,0:T(8,128)S(1)}, f32[2,8,6,16,128]{4,3,2,1,0:T(8,128)}, u32[]{:S(2)}, u32[]{:S(2)}) collective-permute-start(f32[2,8,6,16,128]{4,3,2,1,0:T(8,128)S(1)} %fusion.8), channel_id=1, source_target_pairs={{0,16},{16,32},{24,8},{32,48},{40,24},{48,64},{56,40},{64,80},{72,... | collective-permute-start | bytes 2359304 | tf_op jit(solution)/shard_map/ppermute | solution.py:188
  34.0 4.9 %collective-permute-done.4 = f32[2,8,6,16,128]{4,3,2,1,0:T(8,128)S(1)} collective-permute-done((f32[2,8,6,16,128]{4,3,2,1,0:T(8,128)S(1)}, f32[2,8,6,16,128]{4,3,2,1,0:T(8,128)S(1)}, u32[]{:S(2)}, u32[]{:S(2)}) %collective-permute-start.4) | collective-permute-done | bytes 786464 | tf_op jit(solution)/shard_map/ppermute | solution.py:188
  40.3 2.8 %collective-permute-start.8 = (f32[8,6,16,128]{3,2,1,0:T(8,128)S(1)}, f32[8,6,16,128]{3,2,1,0:T(8,128)S(1)}, u32[]{:S(2)}, u32[]{:S(2)}) collective-permute-start(f32[8,6,16,128]{3,2,1,0:T(8,128)S(1)} %get-tuple-element.23), channel_id=1, source_target_pairs={{0,24},{16,40},{24,0},{32,56},{40,16},{48,72},{56,32},{64,88},{72,... | collective-permute-start | bytes 1179656 | tf_op jit(solution)/shard_map/ppermute | solution.py:188
  43.1 3.9 %collective-permute-start.7 = (f32[8,6,16,128]{3,2,1,0:T(8,128)S(1)}, f32[8,6,16,128]{3,2,1,0:T(8,128)S(1)}, u32[]{:S(2)}, u32[]{:S(2)}) collective-permute-start(f32[8,6,16,128]{3,2,1,0:T(8,128)S(1)} %get-tuple-element.24), channel_id=1, source_target_pairs={{0,16},{16,32},{24,8},{32,48},{40,24},{48,64},{56,40},{64,80},{72,... | collective-permute-start | bytes 1179656 | tf_op jit(solution)/shard_map/ppermute | solution.py:188
  47.5 3.3 %collective-permute-done.8 = f32[8,6,16,128]{3,2,1,0:T(8,128)S(1)} collective-permute-done((f32[8,6,16,128]{3,2,1,0:T(8,128)S(1)}, f32[8,6,16,128]{3,2,1,0:T(8,128)S(1)}, u32[]{:S(2)}, u32[]{:S(2)}) %collective-permute-start.8) | collective-permute-done | bytes 393248 | tf_op jit(solution)/shard_map/ppermute | solution.py:188
  50.8 5.0 %collective-permute-done.7 = f32[8,6,16,128]{3,2,1,0:T(8,128)S(1)} collective-permute-done((f32[8,6,16,128]{3,2,1,0:T(8,128)S(1)}, f32[8,6,16,128]{3,2,1,0:T(8,128)S(1)}, u32[]{:S(2)}, u32[]{:S(2)}) %collective-permute-start.7) | collective-permute-done | bytes 393248 | tf_op jit(solution)/shard_map/ppermute | solution.py:188
  55.8 1.9 %fusion.3 = f32[8,6,16,128]{3,2,1,0:T(8,128)} fusion(f32[8,6,16,128]{3,2,1,0:T(8,128)S(1)} %collective-permute-done.8, f32[8,6,16,128]{3,2,1,0:T(8,128)S(1)} %collective-permute-done.7, f32[3,8,6,32,128]{4,3,2,1,0:T(8,128)} %collective-permute-done, f32[3,8,6,32,128]{4,3,2,1,0:T(8,128)S(1)} %get-tuple-element.14), kind=kLoop, calls=%fused_computation.6 | loop fusion | flops 294912 | bytes 1966080 | tf_op jit(solution)/shard_map/add | solution.py:224
  57.7 10.3 %all-to-all-start.1 = ((f32[8,6,16,128]{3,2,1,0:T(8,128)}), f32[8,6,16,128]{3,2,1,0:T(8,128)S(1)}, u32[]{:S(2)}, u32[]{:S(2)}) async-start(f32[8,6,16,128]{3,2,1,0:T(8,128)} %fusion.3), calls=%async_computation.1 | async-start | bytes 786432 | tf_op jit(solution)/shard_map/all_to_all | solution.py:225
  68.0 1.6 %fusion.5 = (f32[8,6,16,128]{3,2,1,0:T(8,128)S(1)}, f32[8,6,16,128]{3,2,1,0:T(8,128)S(1)}) fusion(f32[3,8,6,32,128]{4,3,2,1,0:T(8,128)} %collective-permute-done, f32[2,8,6,16,128]{4,3,2,1,0:T(8,128)} %collective-permute-done.2, f32[3,8,6,32,128]{4,3,2,1,0:T(8,128)S(1)} %get-tuple-element.14), kind=kLoop, calls=%fused_computation.9 | loop fusion | flops 393216 | bytes 3145728 | tf_op jit(solution)/shard_map/add | solution.py:211
  69.6 3.4 %collective-permute-start.5 = (f32[8,6,16,128]{3,2,1,0:T(8,128)S(1)}, f32[8,6,16,128]{3,2,1,0:T(8,128)S(1)}, u32[]{:S(2)}, u32[]{:S(2)}) collective-permute-start(f32[8,6,16,128]{3,2,1,0:T(8,128)S(1)} %get-tuple-element.26), channel_id=1, source_target_pairs={{0,16},{16,32},{24,8},{32,48},{40,24},{48,64},{56,40},{64,80},{72,... | collective-permute-start | bytes 1179656 | tf_op jit(solution)/shard_map/ppermute | solution.py:188
  73.0 1.9 %collective-permute-start.6 = (f32[8,6,16,128]{3,2,1,0:T(8,128)S(1)}, f32[8,6,16,128]{3,2,1,0:T(8,128)S(1)}, u32[]{:S(2)}, u32[]{:S(2)}) collective-permute-start(f32[8,6,16,128]{3,2,1,0:T(8,128)S(1)} %get-tuple-element.25), channel_id=1, source_target_pairs={{0,24},{16,40},{24,0},{32,56},{40,16},{48,72},{56,32},{64,88},{72,... | collective-permute-start | bytes 1179656 | tf_op jit(solution)/shard_map/ppermute | solution.py:188
  75.0 4.3 %collective-permute-done.5 = f32[8,6,16,128]{3,2,1,0:T(8,128)S(1)} collective-permute-done((f32[8,6,16,128]{3,2,1,0:T(8,128)S(1)}, f32[8,6,16,128]{3,2,1,0:T(8,128)S(1)}, u32[]{:S(2)}, u32[]{:S(2)}) %collective-permute-start.5) | collective-permute-done | bytes 393248 | tf_op jit(solution)/shard_map/ppermute | solution.py:188
  79.3 3.2 %collective-permute-done.6 = f32[8,6,16,128]{3,2,1,0:T(8,128)S(1)} collective-permute-done((f32[8,6,16,128]{3,2,1,0:T(8,128)S(1)}, f32[8,6,16,128]{3,2,1,0:T(8,128)S(1)}, u32[]{:S(2)}, u32[]{:S(2)}) %collective-permute-start.6) | collective-permute-done | bytes 393248 | tf_op jit(solution)/shard_map/ppermute | solution.py:188
  82.5 1.9 %fusion.13 = f32[8,6,16,128]{3,2,1,0:T(8,128)} fusion(f32[8,6,16,128]{3,2,1,0:T(8,128)S(1)} %collective-permute-done.6, f32[8,6,16,128]{3,2,1,0:T(8,128)S(1)} %collective-permute-done.5, f32[3,8,6,32,128]{4,3,2,1,0:T(8,128)} %collective-permute-done, f32[3,8,6,32,128]{4,3,2,1,0:T(8,128)S(1)} %get-tuple-element.14), kind=kLoop, calls=%fused_computation.23 | loop fusion | flops 294912 | bytes 1966080 | tf_op jit(solution)/shard_map/add | solution.py:224
  84.4 7.2 %all-to-all-start = ((f32[8,6,16,128]{3,2,1,0:T(8,128)}), f32[8,6,16,128]{3,2,1,0:T(8,128)S(1)}, u32[]{:S(2)}, u32[]{:S(2)}) async-start(f32[8,6,16,128]{3,2,1,0:T(8,128)} %fusion.13), calls=%async_computation | async-start | bytes 786432 | tf_op jit(solution)/shard_map/all_to_all | solution.py:225
  92.6 14.7 %all-to-all-done = f32[8,6,16,128]{3,2,1,0:T(8,128)S(1)} async-done(((f32[8,6,16,128]{3,2,1,0:T(8,128)}), f32[8,6,16,128]{3,2,1,0:T(8,128)S(1)}, u32[]{:S(2)}, u32[]{:S(2)}) %all-to-all-start) | async-done | bytes 393248 | tf_op jit(solution)/shard_map/all_to_all | solution.py:225
  108.2 12.0 %all_to_all.15 = f32[8,32,128]{2,1,0:T(8,128)S(1)} all-to-all(f32[8,32,128]{2,1,0:T(8,128)S(1)} %shard_map.67), channel_id=1, replica_groups=mesh['dom'=64,'mem'=8] {'mem'}, dimensions={0} | all-to-all | bytes 262144 | tf_op jit(solution)/shard_map/all_to_all | solution.py:232
  (20 shorter events, 9.3 us)
Async XLA Ops:
  0.7 1.9 %copy-start = (bf16[96,128,128]{2,1,0:T(8,128)(2,1)S(1)}, bf16[96,128,128]{2,1,0:T(8,128)(2,1)}, u32[]{:S(2)}) copy-start(bf16[96,128,128]{2,1,0:T(8,128)(2,1)} %weight_hbm.3) | copy-start | bytes 9437188
  2.5 1.4 %copy-start.1 = (bf16[6,32,4096]{2,1,0:T(8,128)(2,1)S(1)}, bf16[6,32,4096]{2,1,0:T(8,128)(2,1)}, u32[]{:S(2)}) copy-start(bf16[6,32,4096]{2,1,0:T(8,128)(2,1)} %ens_hbm.3) | copy-start | bytes 4718596
  4.0 0.7 copy-start.3
  4.6 0.7 copy-start.4
  11.5 27.5 %collective-permute-start = (f32[3,8,6,32,128]{4,3,2,1,0:T(8,128)}, f32[3,8,6,32,128]{4,3,2,1,0:T(8,128)}, u32[]{:S(2)}, u32[]{:S(2)}) collective-permute-start(f32[3,8,6,32,128]{4,3,2,1,0:T(8,128)} %get-tuple-element.15), channel_id=1, source_target_pairs={{0,8},{8,0},{16,24},{24,16},{32,40},{40,32},{48,56},{56,48},{64,72... | collective-permute-start | bytes 7077896 | tf_op jit(solution)/shard_map/ppermute | solution.py:177
  19.6 4.4 %collective-permute-start.3 = (f32[2,8,6,16,128]{4,3,2,1,0:T(8,128)}, f32[2,8,6,16,128]{4,3,2,1,0:T(8,128)S(1)}, u32[]{:S(2)}, u32[]{:S(2)}) collective-permute-start(f32[2,8,6,16,128]{4,3,2,1,0:T(8,128)} %get-tuple-element.18), channel_id=1, source_target_pairs={{0,8},{8,0},{16,24},{24,16},{32,40},{40,32},{48,56},{56,48},{64,72... | collective-permute-start | bytes 2359304 | tf_op jit(solution)/shard_map/ppermute | solution.py:177
  21.6 6.4 %collective-permute-start.1 = (f32[2,8,6,16,128]{4,3,2,1,0:T(8,128)}, f32[2,8,6,16,128]{4,3,2,1,0:T(8,128)S(1)}, u32[]{:S(2)}, u32[]{:S(2)}) collective-permute-start(f32[2,8,6,16,128]{4,3,2,1,0:T(8,128)} %get-tuple-element.16), channel_id=1, source_target_pairs={{0,8},{8,0},{16,24},{24,16},{32,40},{40,32},{48,56},{56,48},{64,72... | collective-permute-start | bytes 2359304 | tf_op jit(solution)/shard_map/ppermute | solution.py:177
  25.1 13.9 %collective-permute-start.4 = (f32[2,8,6,16,128]{4,3,2,1,0:T(8,128)S(1)}, f32[2,8,6,16,128]{4,3,2,1,0:T(8,128)S(1)}, u32[]{:S(2)}, u32[]{:S(2)}) collective-permute-start(f32[2,8,6,16,128]{4,3,2,1,0:T(8,128)S(1)} %fusion.7), channel_id=1, source_target_pairs={{0,16},{16,32},{24,8},{32,48},{40,24},{48,64},{56,40},{64,80},{72,... | collective-permute-start | bytes 2359304 | tf_op jit(solution)/shard_map/ppermute | solution.py:188
  29.1 18.4 %collective-permute-start.2 = (f32[2,8,6,16,128]{4,3,2,1,0:T(8,128)S(1)}, f32[2,8,6,16,128]{4,3,2,1,0:T(8,128)}, u32[]{:S(2)}, u32[]{:S(2)}) collective-permute-start(f32[2,8,6,16,128]{4,3,2,1,0:T(8,128)S(1)} %fusion.8), channel_id=1, source_target_pairs={{0,16},{16,32},{24,8},{32,48},{40,24},{48,64},{56,40},{64,80},{72,... | collective-permute-start | bytes 2359304 | tf_op jit(solution)/shard_map/ppermute | solution.py:188
  40.3 10.5 %collective-permute-start.8 = (f32[8,6,16,128]{3,2,1,0:T(8,128)S(1)}, f32[8,6,16,128]{3,2,1,0:T(8,128)S(1)}, u32[]{:S(2)}, u32[]{:S(2)}) collective-permute-start(f32[8,6,16,128]{3,2,1,0:T(8,128)S(1)} %get-tuple-element.23), channel_id=1, source_target_pairs={{0,24},{16,40},{24,0},{32,56},{40,16},{48,72},{56,32},{64,88},{72,... | collective-permute-start | bytes 1179656 | tf_op jit(solution)/shard_map/ppermute | solution.py:188
  43.1 12.8 %collective-permute-start.7 = (f32[8,6,16,128]{3,2,1,0:T(8,128)S(1)}, f32[8,6,16,128]{3,2,1,0:T(8,128)S(1)}, u32[]{:S(2)}, u32[]{:S(2)}) collective-permute-start(f32[8,6,16,128]{3,2,1,0:T(8,128)S(1)} %get-tuple-element.24), channel_id=1, source_target_pairs={{0,16},{16,32},{24,8},{32,48},{40,24},{48,64},{56,40},{64,80},{72,... | collective-permute-start | bytes 1179656 | tf_op jit(solution)/shard_map/ppermute | solution.py:188
  57.7 26.7 %all-to-all-start.1 = ((f32[8,6,16,128]{3,2,1,0:T(8,128)}), f32[8,6,16,128]{3,2,1,0:T(8,128)S(1)}, u32[]{:S(2)}, u32[]{:S(2)}) async-start(f32[8,6,16,128]{3,2,1,0:T(8,128)} %fusion.3), calls=%async_computation.1 | async-start | bytes 786432 | tf_op jit(solution)/shard_map/all_to_all | solution.py:225
  68.0 23.6 %copy-start.2 = (f32[32,1024]{1,0:T(8,128)S(1)}, f32[32,1024]{1,0:T(8,128)}, u32[]{:S(2)}) copy-start(f32[32,1024]{1,0:T(8,128)} %observed_ref.3) | copy-start | bytes 393220
  69.6 9.7 %collective-permute-start.5 = (f32[8,6,16,128]{3,2,1,0:T(8,128)S(1)}, f32[8,6,16,128]{3,2,1,0:T(8,128)S(1)}, u32[]{:S(2)}, u32[]{:S(2)}) collective-permute-start(f32[8,6,16,128]{3,2,1,0:T(8,128)S(1)} %get-tuple-element.26), channel_id=1, source_target_pairs={{0,16},{16,32},{24,8},{32,48},{40,24},{48,64},{56,40},{64,80},{72,... | collective-permute-start | bytes 1179656 | tf_op jit(solution)/shard_map/ppermute | solution.py:188
  73.0 9.5 %collective-permute-start.6 = (f32[8,6,16,128]{3,2,1,0:T(8,128)S(1)}, f32[8,6,16,128]{3,2,1,0:T(8,128)S(1)}, u32[]{:S(2)}, u32[]{:S(2)}) collective-permute-start(f32[8,6,16,128]{3,2,1,0:T(8,128)S(1)} %get-tuple-element.25), channel_id=1, source_target_pairs={{0,24},{16,40},{24,0},{32,56},{40,16},{48,72},{56,32},{64,88},{72,... | collective-permute-start | bytes 1179656 | tf_op jit(solution)/shard_map/ppermute | solution.py:188
  84.4 22.8 %all-to-all-start = ((f32[8,6,16,128]{3,2,1,0:T(8,128)}), f32[8,6,16,128]{3,2,1,0:T(8,128)S(1)}, u32[]{:S(2)}, u32[]{:S(2)}) async-start(f32[8,6,16,128]{3,2,1,0:T(8,128)} %fusion.13), calls=%async_computation | async-start | bytes 786432 | tf_op jit(solution)/shard_map/all_to_all | solution.py:225
where the time goes:
time: 122 us; the launch traced here: 121 us
  starting transfers between devices  43.6 us (36%)
  waiting for transfers between devices  36.1 us (30%)
  Pallas kernels  14.3 us (12%)
  blocking collectives  12 us (10%)
  other arithmetic  8.85 us (7%)
  local copies, waits for them, and re-layouts  5.27 us (4%)
    ppermute x6, waiting for transfers between devices, passed_on(): return lax.ppermute(value, 'dom', pairs)  21.3 us
    ppermute x6, starting transfers between devices, passed_on(): return lax.ppermute(value, 'dom', pairs)  19.9 us
    all_to_all x2, starting transfers between devices, on_device(): lax.all_to_all(summed, 'mem', split_axis=0, concat_axis=0, tiled=True)  17.5 us
    all_to_all x2, waiting for transfers between devices, on_device(): lax.all_to_all(summed, 'mem', split_axis=0, concat_axis=0, tiled=True)  14.7 us
    pallas_call x2, Pallas kernels, remap(): pl.pallas_call(functools.partial(remap_kernel, coded(table), parts, split...  12.4 us
    all_to_all x1, blocking collectives, on_device(): lax.all_to_all(copies, 'mem', split_axis=0, concat_axis=0, tiled=True)  12 us
    ppermute x3, starting transfers between devices, swapped(): lax.ppermute(value, 'dom', [(source, source ^ 1) for source in range(coun...  6.25 us
    unnamed x10, local copies, waits for them, and re-layouts  4.61 us
  transfers between devices with their start and end apart: 11, of which 7 were waited for; matrix products, arithmetic and copies ran while one was open for 6% of the time, Pallas kernels for 6%

commit v1 on v0

--- a/solution.py
+++ b/solution.py
@@ -19,21 +19,27 @@
     return sum(table.get(u, 7) << (3 * (u + 4)) for u in range(-4, 5))
 
 
-def remap_kernel(codes, parts, split, chunks, block_hbm, target_hbm, count_hbm, ens_hbm, weight_hbm, *rest):
-    outs, (acc, ens, weights, blocks, targets, count, slots, sems) = rest[:-8], rest[-8:]
-    groups, levels, _ = ens.shape
+def remap_kernel(codes, parts, load, block_hbm, target_hbm, count_hbm, ens_in, weight_in, *rest):
+    outs, (acc, blocks, targets, count, slots, sems) = rest[:-6], rest[-6:]
+    ens, weights = ens_in, weight_in
+    if load:
+        *outs, ens, weights = outs
+    groups, levels, _ = ens_in.shape
     total = targets.shape[0]
     owned = 8
     small = [
         pltpu.make_async_copy(source, target, sems.at[index])
         for index, (source, target) in enumerate(((target_hbm, targets), (count_hbm, count), (block_hbm, blocks)))
     ]
-    large = [pltpu.make_async_copy(ens_hbm.at[group], ens.at[group], sems.at[3 + group]) for group in range(groups)]
-    pieces = 4
-    span = total // pieces
-    for piece in range(pieces):
-        part = pl.ds(piece * span, span)
-        large.append(pltpu.make_async_copy(weight_hbm.at[part], weights.at[part], sems.at[3 + groups + piece]))
+    large = []
+    if load:
+        pieces = 4
+        span = total // pieces
+        for group in range(groups):
+            large.append(pltpu.make_async_copy(ens_in.at[group], ens.at[group], sems.at[3 + group]))
+        for piece in range(pieces):
+            part = pl.ds(piece * span, span)
+            large.append(pltpu.make_async_copy(weight_in.at[part], weights.at[part], sems.at[3 + groups + piece]))
     for copy in small + large:
         copy.start()
     device = lax.axis_index("dom")
@@ -79,34 +85,33 @@
     lax.fori_loop(0, (found + UNROLL - 1) // UNROLL, added, 0)
 
     def stored(tile, carry):
-        start = 0
-        for index, length in enumerate(chunks):
-            for low, high, out in ((0, split, outs[2 * index]), (split, parts, outs[2 * index + 1])):
-                for part in range(low, high):
-                    for group in range(groups):
-                        out[part - low, tile, group] = acc[part * owned + tile, pl.ds(group * levels + start, length)]
-            start += length
+        part = 0
+        for out in outs:
+            for place in range(out.shape[0]):
+                for group in range(groups):
+                    out[place, tile, group] = acc[part * owned + tile, pl.ds(group * levels, levels)]
+                part += 1
         return carry
 
     lax.fori_loop(0, owned, stored, 0)
 
 
-def remap(table, parts, split, chunks, limit, ensemble, tile_weight, tile_block, tile_target, tile_count):
+def remap(table, splits, load, ensemble, tile_weight, tile_block, tile_target, tile_count):
     groups, levels, _ = ensemble.shape
     slots = tile_block.shape[0]
-    shapes = []
-    for length in chunks:
-        for count in (split, parts - split):
-            shapes.append(jax.ShapeDtypeStruct((count, 8, groups, length, 128), jnp.float32))
-    outs = pl.pallas_call(
-        functools.partial(remap_kernel, coded(table), parts, split, chunks),
+    parts = sum(splits)
+    shapes = [jax.ShapeDtypeStruct((count, 8, groups, levels, 128), jnp.float32) for count in splits]
+    if load:
+        shapes += [jax.ShapeDtypeStruct(value.shape, value.dtype) for value in (ensemble, tile_weight)]
+    hbm = pl.BlockSpec(memory_space=pltpu.HBM)
+    vmem = pl.BlockSpec(memory_space=pltpu.VMEM)
+    return pl.pallas_call(
+        functools.partial(remap_kernel, coded(table), parts, load),
         out_shape=shapes,
-        in_specs=[pl.BlockSpec(memory_space=pltpu.HBM)] * 5,
-        out_specs=[pl.BlockSpec(memory_space=pltpu.VMEM)] * len(shapes),
+        in_specs=[hbm] * 3 + [hbm if load else vmem] * 2,
+        out_specs=[vmem] * len(shapes),
         scratch_shapes=[
             pltpu.VMEM((parts * 8 + 1, groups * levels, 128), jnp.float32),
-            pltpu.VMEM(ensemble.shape, ensemble.dtype),
-            pltpu.VMEM(tile_weight.shape, tile_weight.dtype),
             pltpu.SMEM((slots,), jnp.int32),
             pltpu.SMEM((slots,), jnp.int32),
             pltpu.SMEM((1,), jnp.int32),
@@ -116,9 +121,8 @@
         cost_estimate=pl.CostEstimate(
             flops=2 * slots * groups * levels * 128 * 128, bytes_accessed=12_000_000, transcendentals=0
         ),
-        compiler_params=pltpu.CompilerParams(vmem_limit_bytes=limit * 1024 * 1024),
+        compiler_params=pltpu.CompilerParams(vmem_limit_bytes=18 * 1024 * 1024),
     )(tile_block, tile_target, tile_count, ensemble, tile_weight)
-    return [outs[2 * index : 2 * index + 2] for index in range(len(chunks))]
 
 
 def score_kernel(first, copies, members_ref, observed_ref, *rest):
@@ -189,16 +193,21 @@
 
 
 def on_device(ensemble, observed, tile_weight, tile_block, tile_target, tile_count):
-    groups, levels, _ = ensemble.shape
+    groups, _, _ = ensemble.shape
     tiles = (ensemble, tile_weight, tile_block, tile_target, tile_count)
-    far = remap(FAR, 3, 1, CHUNKS, 61, *tiles)
+    tiles = tuple(pltpu.with_memory_space_constraint(value, pltpu.HBM) for value in tiles[:4]) + tiles[4:]
+    keep, give, *held = remap(FAR, (1, 2), True, *tiles)
+    from_core = swapped(give)
     ahead = []
-    for keep, give in far:
-        from_core = swapped(give)
-        message = lax.dynamic_update_slice_in_dim(from_core, from_core[:1] + keep, 0, 0)
-        ahead.append(passed_on(message, False))
-    ((keep, give),) = remap(NEAR, 6, 3, (levels,), 18, *tiles)
+    first = 0
+    for length in CHUNKS:
+        part = slice(first, first + length)
+        value = jnp.concatenate([from_core[:1, :, :, part] + keep[:, :, :, part], from_core[1:, :, :, part]])
+        ahead.append(passed_on(value, False))
+        first += length
+    keep, own, give = remap(NEAR, (2, 1, 3), False, *held, *tiles[2:])
     from_core = swapped(give)
+    here = own[0] + from_core[2]
     hops = []
     first = 0
     before = None
@@ -221,7 +230,7 @@
         arrived = hops[index]
         if index:
             arrived, before = lax.optimization_barrier((arrived, summed))
-        summed = keep[2, :, :, part] + from_core[2, :, :, part] + arrived[0] + arrived[1]
+        summed = here[:, :, part] + arrived[0] + arrived[1]
         regrouped = lax.all_to_all(summed, "mem", split_axis=0, concat_axis=0, tiled=True)
         regrouped = regrouped.reshape(8 * groups, length, 128)
         if index + 1 < len(CHUNKS):

time: 122 us -> 110 us (0.902)
  the two profiles are of different devices: /device:TPU:18 before, /device:TPU:7 now
where the time goes in v1:
time: 110 us; the launch traced here: 109 us
  starting transfers between devices  46.7 us (42%)
  waiting for transfers between devices  34.5 us (31%)
  blocking collectives  12 us (11%)
  Pallas kernels  11 us (10%)
  other arithmetic  3.68 us (3%)
    ppermute x6, starting transfers between devices, passed_on(): return lax.ppermute(value, 'dom', pairs)  25.6 us
    ppermute x6, waiting for transfers between devices, passed_on(): return lax.ppermute(value, 'dom', pairs)  21.9 us
    all_to_all x2, starting transfers between devices, on_device(): lax.all_to_all(summed, 'mem', split_axis=0, concat_axis=0, tiled=True)  17 us
    all_to_all x2, waiting for transfers between devices, on_device(): lax.all_to_all(summed, 'mem', split_axis=0, concat_axis=0, tiled=True)  12.6 us
    all_to_all x1, blocking collectives, on_device(): lax.all_to_all(copies, 'mem', split_axis=0, concat_axis=0, tiled=True)  12 us
    pallas_call x2, Pallas kernels, remap(): pl.pallas_call(functools.partial(remap_kernel, coded(table), parts, load)...  9.06 us
    ppermute x2, starting transfers between devices, swapped(): lax.ppermute(value, 'dom', [(source, source ^ 1) for source in range(coun...  4.08 us
  transfers between devices with their start and end apart: 10, of which 6 were waited for; matrix products, arithmetic and copies ran while one was open for 3% of the time, Pallas kernels for 5%

profile of v1, /device:TPU:7, one launch (start us, length us, event | category | flops | bytes accessed | tf_op | source)
XLA Modules:
  0.0 109.3 jit_solution(4703479234432730792)
XLA Ops:
  0.7 4.3 %shard_map.64 = (f32[1,8,6,32,128]{4,3,2,1,0:T(8,128)S(1)}, f32[2,8,6,32,128]{4,3,2,1,0:T(8,128)S(1)}, bf16[6,32,4096]{2,1,0:T(8,128)(2,1)S(1)}, bf16[96,128,128]{2,1,0:T(8,128)(2,1)S(1)}) custom-call(s32[96]{0:T(128)} %block_hbm.3, s32[96]{0:T(128)} %target_hbm.3, s32[1]{0:T(128)S(6)} %copy.10.count_hbm, bf16[6,32,4096]{2,1,0:T(8,128)(2,1)} %ens_in.1, ...), custom_call_target="tpu_custom_call" | custom-call | flops 603979776 | bytes 12000000 | tf_op jit(solution)/shard_map/pallas_call | solution.py:108
  5.0 2.2 %collective-permute-start.1 = (f32[2,8,6,32,128]{4,3,2,1,0:T(8,128)S(1)}, f32[2,8,6,32,128]{4,3,2,1,0:T(8,128)S(1)}, u32[]{:S(2)}, u32[]{:S(2)}) collective-permute-start(f32[2,8,6,32,128]{4,3,2,1,0:T(8,128)S(1)} %get-tuple-element.20), channel_id=1, source_target_pairs={{0,8},{8,0},{16,24},{24,16},{32,40},{40,32},{48,56},{56,48},{64,72... | collective-permute-start | bytes 4718600 | tf_op jit(solution)/shard_map/ppermute | solution.py:181
  7.1 4.8 %shard_map.65 = (f32[2,8,6,32,128]{4,3,2,1,0:T(8,128)S(1)}, f32[1,8,6,32,128]{4,3,2,1,0:T(8,128)S(1)}, f32[3,8,6,32,128]{4,3,2,1,0:T(8,128)S(1)}) custom-call(s32[96]{0:T(128)} %block_hbm.3, s32[96]{0:T(128)} %target_hbm.3, s32[1]{0:T(128)S(6)} %copy.10.count_hbm, bf16[6,32,4096]{2,1,0:T(8,128)(2,1)S(1)} %get-tuple-element.15.ens_in, ...), custom_call_target="tpu_custom_call" | custom-call | flops 603979776 | bytes 12000000 | tf_op jit(solution)/shard_map/pallas_call | solution.py:108
  11.9 1.9 %collective-permute-start = (f32[3,8,6,32,128]{4,3,2,1,0:T(8,128)S(1)}, f32[3,8,6,32,128]{4,3,2,1,0:T(8,128)S(1)}, u32[]{:S(2)}, u32[]{:S(2)}) collective-permute-start(f32[3,8,6,32,128]{4,3,2,1,0:T(8,128)S(1)} %get-tuple-element.18), channel_id=1, source_target_pairs={{0,8},{8,0},{16,24},{24,16},{32,40},{40,32},{48,56},{56,48},{64,72... | collective-permute-start | bytes 7077896 | tf_op jit(solution)/shard_map/ppermute | solution.py:181
  14.1 5.8 %collective-permute-start.3 = (f32[2,8,6,16,128]{4,3,2,1,0:T(8,128)S(1)}, f32[2,8,6,16,128]{4,3,2,1,0:T(8,128)S(1)}, u32[]{:S(2)}, u32[]{:S(2)}) collective-permute-start(f32[2,8,6,16,128]{4,3,2,1,0:T(8,128)S(1)} %pad_maximum_fusion.1), channel_id=1, source_target_pairs={{0,16},{16,32},{24,8},{32,48},{40,24},{48,64},{56,40},{64,80},{72,... | collective-permute-start | bytes 2359304 | tf_op jit(solution)/shard_map/ppermute | solution.py:192
  19.9 2.8 %collective-permute-start.2 = (f32[2,8,6,16,128]{4,3,2,1,0:T(8,128)S(1)}, f32[2,8,6,16,128]{4,3,2,1,0:T(8,128)S(1)}, u32[]{:S(2)}, u32[]{:S(2)}) collective-permute-start(f32[2,8,6,16,128]{4,3,2,1,0:T(8,128)S(1)} %pad_maximum_fusion), channel_id=1, source_target_pairs={{0,16},{16,32},{24,8},{32,48},{40,24},{48,64},{56,40},{64,80},{72,... | collective-permute-start | bytes 2359304 | tf_op jit(solution)/shard_map/ppermute | solution.py:192
  22.7 6.1 %collective-permute-done.3 = f32[2,8,6,16,128]{4,3,2,1,0:T(8,128)S(1)} collective-permute-done((f32[2,8,6,16,128]{4,3,2,1,0:T(8,128)S(1)}, f32[2,8,6,16,128]{4,3,2,1,0:T(8,128)S(1)}, u32[]{:S(2)}, u32[]{:S(2)}) %collective-permute-start.3) | collective-permute-done | bytes 786464 | tf_op jit(solution)/shard_map/ppermute | solution.py:192
  29.0 5.9 %collective-permute-start.6 = (f32[8,6,16,128]{3,2,1,0:T(8,128)S(1)}, f32[8,6,16,128]{3,2,1,0:T(8,128)S(1)}, u32[]{:S(2)}, u32[]{:S(2)}) collective-permute-start(f32[8,6,16,128]{3,2,1,0:T(8,128)S(1)} %get-tuple-element.26), channel_id=1, source_target_pairs={{0,16},{16,32},{24,8},{32,48},{40,24},{48,64},{56,40},{64,80},{72,... | collective-permute-start | bytes 1179656 | tf_op jit(solution)/shard_map/ppermute | solution.py:192
  34.9 3.5 %collective-permute-start.7 = (f32[8,6,16,128]{3,2,1,0:T(8,128)S(1)}, f32[8,6,16,128]{3,2,1,0:T(8,128)S(1)}, u32[]{:S(2)}, u32[]{:S(2)}) collective-permute-start(f32[8,6,16,128]{3,2,1,0:T(8,128)S(1)} %get-tuple-element.25), channel_id=1, source_target_pairs={{0,24},{16,40},{24,0},{32,56},{40,16},{48,72},{56,32},{64,88},{72,... | collective-permute-start | bytes 1179656 | tf_op jit(solution)/shard_map/ppermute | solution.py:192
  38.6 2.8 %collective-permute-done.6 = f32[8,6,16,128]{3,2,1,0:T(8,128)S(1)} collective-permute-done((f32[8,6,16,128]{3,2,1,0:T(8,128)S(1)}, f32[8,6,16,128]{3,2,1,0:T(8,128)S(1)}, u32[]{:S(2)}, u32[]{:S(2)}) %collective-permute-start.6) | collective-permute-done | bytes 393248 | tf_op jit(solution)/shard_map/ppermute | solution.py:192
  41.4 5.3 %collective-permute-done.7 = f32[8,6,16,128]{3,2,1,0:T(8,128)S(1)} collective-permute-done((f32[8,6,16,128]{3,2,1,0:T(8,128)S(1)}, f32[8,6,16,128]{3,2,1,0:T(8,128)S(1)}, u32[]{:S(2)}, u32[]{:S(2)}) %collective-permute-start.7) | collective-permute-done | bytes 393248 | tf_op jit(solution)/shard_map/ppermute | solution.py:192
  46.7 0.8 fusion.2
  47.6 10.0 %all-to-all-start.1 = ((f32[8,6,16,128]{3,2,1,0:T(8,128)}), f32[8,6,16,128]{3,2,1,0:T(8,128)S(1)}, u32[]{:S(2)}, u32[]{:S(2)}) async-start(f32[8,6,16,128]{3,2,1,0:T(8,128)} %fusion.2), calls=%async_computation.1 | async-start | bytes 786432 | tf_op jit(solution)/shard_map/all_to_all | solution.py:234
  57.6 1.3 %fusion.4 = (f32[8,6,16,128]{3,2,1,0:T(8,128)S(1)}, f32[8,6,16,128]{3,2,1,0:T(8,128)S(1)}) fusion(f32[3,8,6,32,128]{4,3,2,1,0:T(8,128)} %copy-done.1, f32[2,8,6,16,128]{4,3,2,1,0:T(8,128)S(1)} %collective-permute-done.2, f32[2,8,6,32,128]{4,3,2,1,0:T(8,128)S(1)} %get-tuple-element.19), kind=kLoop, calls=%fused_computation.11 | loop fusion | flops 393216 | bytes 3145728 | tf_op jit(solution)/shard_map/add | solution.py:220
  58.9 4.1 %collective-permute-start.4 = (f32[8,6,16,128]{3,2,1,0:T(8,128)S(1)}, f32[8,6,16,128]{3,2,1,0:T(8,128)S(1)}, u32[]{:S(2)}, u32[]{:S(2)}) collective-permute-start(f32[8,6,16,128]{3,2,1,0:T(8,128)S(1)} %get-tuple-element.28), channel_id=1, source_target_pairs={{0,16},{16,32},{24,8},{32,48},{40,24},{48,64},{56,40},{64,80},{72,... | collective-permute-start | bytes 1179656 | tf_op jit(solution)/shard_map/ppermute | solution.py:192
  63.0 3.6 %collective-permute-start.5 = (f32[8,6,16,128]{3,2,1,0:T(8,128)S(1)}, f32[8,6,16,128]{3,2,1,0:T(8,128)S(1)}, u32[]{:S(2)}, u32[]{:S(2)}) collective-permute-start(f32[8,6,16,128]{3,2,1,0:T(8,128)S(1)} %get-tuple-element.27), channel_id=1, source_target_pairs={{0,24},{16,40},{24,0},{32,56},{40,16},{48,72},{56,32},{64,88},{72,... | collective-permute-start | bytes 1179656 | tf_op jit(solution)/shard_map/ppermute | solution.py:192
  66.7 1.2 %collective-permute-done.4 = f32[8,6,16,128]{3,2,1,0:T(8,128)S(1)} collective-permute-done((f32[8,6,16,128]{3,2,1,0:T(8,128)S(1)}, f32[8,6,16,128]{3,2,1,0:T(8,128)S(1)}, u32[]{:S(2)}, u32[]{:S(2)}) %collective-permute-start.4) | collective-permute-done | bytes 393248 | tf_op jit(solution)/shard_map/ppermute | solution.py:192
  67.9 6.5 %collective-permute-done.5 = f32[8,6,16,128]{3,2,1,0:T(8,128)S(1)} collective-permute-done((f32[8,6,16,128]{3,2,1,0:T(8,128)S(1)}, f32[8,6,16,128]{3,2,1,0:T(8,128)S(1)}, u32[]{:S(2)}, u32[]{:S(2)}) %collective-permute-start.5) | collective-permute-done | bytes 393248 | tf_op jit(solution)/shard_map/ppermute | solution.py:192
  74.4 0.8 fusion.8
  75.2 6.9 %all-to-all-start = ((f32[8,6,16,128]{3,2,1,0:T(8,128)}), f32[8,6,16,128]{3,2,1,0:T(8,128)S(1)}, u32[]{:S(2)}, u32[]{:S(2)}) async-start(f32[8,6,16,128]{3,2,1,0:T(8,128)} %fusion.8), calls=%async_computation | async-start | bytes 786432 | tf_op jit(solution)/shard_map/all_to_all | solution.py:234
  82.2 0.9 shard_map.66.rest_0_
  83.1 12.6 %all-to-all-done = f32[8,6,16,128]{3,2,1,0:T(8,128)S(1)} async-done(((f32[8,6,16,128]{3,2,1,0:T(8,128)}), f32[8,6,16,128]{3,2,1,0:T(8,128)S(1)}, u32[]{:S(2)}, u32[]{:S(2)}) %all-to-all-start) | async-done | bytes 393248 | tf_op jit(solution)/shard_map/all_to_all | solution.py:234
  95.7 1.0 shard_map.67
  96.6 12.0 %all_to_all.15 = f32[8,32,128]{2,1,0:T(8,128)S(1)} all-to-all(f32[8,32,128]{2,1,0:T(8,128)S(1)} %shard_map.67), channel_id=1, replica_groups=mesh['dom'=64,'mem'=8] {'mem'}, dimensions={0} | all-to-all | bytes 262144 | tf_op jit(solution)/shard_map/all_to_all | solution.py:241
  (14 shorter events, 1.4 us)
Async XLA Ops:
  5.0 8.9 %collective-permute-start.1 = (f32[2,8,6,32,128]{4,3,2,1,0:T(8,128)S(1)}, f32[2,8,6,32,128]{4,3,2,1,0:T(8,128)S(1)}, u32[]{:S(2)}, u32[]{:S(2)}) collective-permute-start(f32[2,8,6,32,128]{4,3,2,1,0:T(8,128)S(1)} %get-tuple-element.20), channel_id=1, source_target_pairs={{0,8},{8,0},{16,24},{24,16},{32,40},{40,32},{48,56},{56,48},{64,72... | collective-permute-start | bytes 4718600 | tf_op jit(solution)/shard_map/ppermute | solution.py:181
  11.9 16.9 %collective-permute-start = (f32[3,8,6,32,128]{4,3,2,1,0:T(8,128)S(1)}, f32[3,8,6,32,128]{4,3,2,1,0:T(8,128)S(1)}, u32[]{:S(2)}, u32[]{:S(2)}) collective-permute-start(f32[3,8,6,32,128]{4,3,2,1,0:T(8,128)S(1)} %get-tuple-element.18), channel_id=1, source_target_pairs={{0,8},{8,0},{16,24},{24,16},{32,40},{40,32},{48,56},{56,48},{64,72... | collective-permute-start | bytes 7077896 | tf_op jit(solution)/shard_map/ppermute | solution.py:181
  14.1 14.7 %collective-permute-start.3 = (f32[2,8,6,16,128]{4,3,2,1,0:T(8,128)S(1)}, f32[2,8,6,16,128]{4,3,2,1,0:T(8,128)S(1)}, u32[]{:S(2)}, u32[]{:S(2)}) collective-permute-start(f32[2,8,6,16,128]{4,3,2,1,0:T(8,128)S(1)} %pad_maximum_fusion.1), channel_id=1, source_target_pairs={{0,16},{16,32},{24,8},{32,48},{40,24},{48,64},{56,40},{64,80},{72,... | collective-permute-start | bytes 2359304 | tf_op jit(solution)/shard_map/ppermute | solution.py:192
  19.9 18.5 %collective-permute-start.2 = (f32[2,8,6,16,128]{4,3,2,1,0:T(8,128)S(1)}, f32[2,8,6,16,128]{4,3,2,1,0:T(8,128)S(1)}, u32[]{:S(2)}, u32[]{:S(2)}) collective-permute-start(f32[2,8,6,16,128]{4,3,2,1,0:T(8,128)S(1)} %pad_maximum_fusion), channel_id=1, source_target_pairs={{0,16},{16,32},{24,8},{32,48},{40,24},{48,64},{56,40},{64,80},{72,... | collective-permute-start | bytes 2359304 | tf_op jit(solution)/shard_map/ppermute | solution.py:192
  28.8 9.7 %copy-start.1 = (f32[3,8,6,32,128]{4,3,2,1,0:T(8,128)}, f32[3,8,6,32,128]{4,3,2,1,0:T(8,128)S(1)}, u32[]{:S(2)}) copy-start(f32[3,8,6,32,128]{4,3,2,1,0:T(8,128)S(1)} %collective-permute-done) | copy-start | bytes 7077892
  29.0 12.4 %collective-permute-start.6 = (f32[8,6,16,128]{3,2,1,0:T(8,128)S(1)}, f32[8,6,16,128]{3,2,1,0:T(8,128)S(1)}, u32[]{:S(2)}, u32[]{:S(2)}) collective-permute-start(f32[8,6,16,128]{3,2,1,0:T(8,128)S(1)} %get-tuple-element.26), channel_id=1, source_target_pairs={{0,16},{16,32},{24,8},{32,48},{40,24},{48,64},{56,40},{64,80},{72,... | collective-permute-start | bytes 1179656 | tf_op jit(solution)/shard_map/ppermute | solution.py:192
  34.9 11.8 %collective-permute-start.7 = (f32[8,6,16,128]{3,2,1,0:T(8,128)S(1)}, f32[8,6,16,128]{3,2,1,0:T(8,128)S(1)}, u32[]{:S(2)}, u32[]{:S(2)}) collective-permute-start(f32[8,6,16,128]{3,2,1,0:T(8,128)S(1)} %get-tuple-element.25), channel_id=1, source_target_pairs={{0,24},{16,40},{24,0},{32,56},{40,16},{48,72},{56,32},{64,88},{72,... | collective-permute-start | bytes 1179656 | tf_op jit(solution)/shard_map/ppermute | solution.py:192
  47.6 27.7 %all-to-all-start.1 = ((f32[8,6,16,128]{3,2,1,0:T(8,128)}), f32[8,6,16,128]{3,2,1,0:T(8,128)S(1)}, u32[]{:S(2)}, u32[]{:S(2)}) async-start(f32[8,6,16,128]{3,2,1,0:T(8,128)} %fusion.2), calls=%async_computation.1 | async-start | bytes 786432 | tf_op jit(solution)/shard_map/all_to_all | solution.py:234
  58.9 23.2 %copy-start = (f32[32,1024]{1,0:T(8,128)S(1)}, f32[32,1024]{1,0:T(8,128)}, u32[]{:S(2)}) copy-start(f32[32,1024]{1,0:T(8,128)} %observed_ref.3) | copy-start | bytes 393220
  58.9 8.9 %collective-permute-start.4 = (f32[8,6,16,128]{3,2,1,0:T(8,128)S(1)}, f32[8,6,16,128]{3,2,1,0:T(8,128)S(1)}, u32[]{:S(2)}, u32[]{:S(2)}) collective-permute-start(f32[8,6,16,128]{3,2,1,0:T(8,128)S(1)} %get-tuple-element.28), channel_id=1, source_target_pairs={{0,16},{16,32},{24,8},{32,48},{40,24},{48,64},{56,40},{64,80},{72,... | collective-permute-start | bytes 1179656 | tf_op jit(solution)/shard_map/ppermute | solution.py:192
  63.0 11.4 %collective-permute-start.5 = (f32[8,6,16,128]{3,2,1,0:T(8,128)S(1)}, f32[8,6,16,128]{3,2,1,0:T(8,128)S(1)}, u32[]{:S(2)}, u32[]{:S(2)}) collective-permute-start(f32[8,6,16,128]{3,2,1,0:T(8,128)S(1)} %get-tuple-element.27), channel_id=1, source_target_pairs={{0,24},{16,40},{24,0},{32,56},{40,16},{48,72},{56,32},{64,88},{72,... | collective-permute-start | bytes 1179656 | tf_op jit(solution)/shard_map/ppermute | solution.py:192
  75.2 20.4 %all-to-all-start = ((f32[8,6,16,128]{3,2,1,0:T(8,128)}), f32[8,6,16,128]{3,2,1,0:T(8,128)S(1)}, u32[]{:S(2)}, u32[]{:S(2)}) async-start(f32[8,6,16,128]{3,2,1,0:T(8,128)} %fusion.8), calls=%async_computation | async-start | bytes 786432 | tf_op jit(solution)/shard_map/all_to_all | solution.py:234

commit v2 on v1

--- a/solution.py
+++ b/solution.py
@@ -8,7 +8,7 @@
 from jax.sharding import PartitionSpec as P
 
 
-CHUNKS = (16, 16)
+CHUNKS = (8, 24)
 
 FAR = {4: 0, -3: 1, -4: 2}
 NEAR = {2: 0, 3: 1, 0: 2, -1: 3, -2: 4, 1: 5}
@@ -121,7 +121,7 @@
         cost_estimate=pl.CostEstimate(
             flops=2 * slots * groups * levels * 128 * 128, bytes_accessed=12_000_000, transcendentals=0
         ),
-        compiler_params=pltpu.CompilerParams(vmem_limit_bytes=18 * 1024 * 1024),
+        compiler_params=pltpu.CompilerParams(vmem_limit_bytes=16 * 1024 * 1024),
     )(tile_block, tile_target, tile_count, ensemble, tile_weight)
 
 
@@ -172,7 +172,7 @@
         cost_estimate=pl.CostEstimate(
             flops=3 * count * count * length * cells // 2, bytes_accessed=4 * count * length * cells, transcendentals=0
         ),
-        compiler_params=pltpu.CompilerParams(vmem_limit_bytes=16 * 1024 * 1024),
+        compiler_params=pltpu.CompilerParams(vmem_limit_bytes=8 * 1024 * 1024),
     )(members, observed, *before)
 
 
@@ -193,7 +193,7 @@
 
 
 def on_device(ensemble, observed, tile_weight, tile_block, tile_target, tile_count):
-    groups, _, _ = ensemble.shape
+    groups, levels, _ = ensemble.shape
     tiles = (ensemble, tile_weight, tile_block, tile_target, tile_count)
     tiles = tuple(pltpu.with_memory_space_constraint(value, pltpu.HBM) for value in tiles[:4]) + tiles[4:]
     keep, give, *held = remap(FAR, (1, 2), True, *tiles)
@@ -207,37 +207,41 @@
         first += length
     keep, own, give = remap(NEAR, (2, 1, 3), False, *held, *tiles[2:])
     from_core = swapped(give)
-    here = own[0] + from_core[2]
-    hops = []
-    first = 0
-    before = None
-    for index, length in enumerate(CHUNKS):
-        part = slice(first, first + length)
-        farther = ahead[index]
-        if index:
-            farther, before = lax.optimization_barrier((farther, before))
-        same = keep[0, :, :, part] + from_core[0, :, :, part] + farther[0]
-        cross = keep[1, :, :, part] + from_core[1, :, :, part] + farther[1]
-        before = same
+    here, nearby = lax.optimization_barrier((own[0] + from_core[2], keep + from_core[:2]))
+
+    def led(index, first):
+        part = slice(first, first + CHUNKS[index])
+        return [nearby[way, :, :, part] + ahead[index][way] for way in (0, 1)]
+
+    turned = CHUNKS[0]
+    both = led(0, 0)
+    both = jnp.stack([*both, here[:, :, :turned]], axis=1)
+    mixed = lax.all_to_all(both, "mem", split_axis=0, concat_axis=0, tiled=True)
+    before = both
+    first = turned
+    starts = []
+    for index in range(1, len(CHUNKS)):
+        ahead[index], before = lax.optimization_barrier((ahead[index], before))
+        before = led(index, first)
+        starts.append(before)
+        first += CHUNKS[index]
+    first = turned
+    arrived = []
+    for index, (same, cross) in enumerate(starts, 1):
         same = passed_on(same, False)
         cross = passed_on(cross, True)
-        hops.append((same, cross))
-        first += length
-    scores = []
-    first = 0
-    for index, length in enumerate(CHUNKS):
-        part = slice(first, first + length)
-        arrived = hops[index]
-        if index:
-            arrived, before = lax.optimization_barrier((arrived, summed))
-        summed = here[:, :, part] + arrived[0] + arrived[1]
-        regrouped = lax.all_to_all(summed, "mem", split_axis=0, concat_axis=0, tiled=True)
-        regrouped = regrouped.reshape(8 * groups, length, 128)
-        if index + 1 < len(CHUNKS):
-            scores.append(scored(first, regrouped, observed))
-        else:
-            copies = scored(first, regrouped, observed, scores, lax.axis_size("mem"))
-        first += length
+        arrived.append((same, cross, here[:, :, first : first + CHUNKS[index]]))
+        first += CHUNKS[index]
+    same, cross, rest = (mixed[:, way] for way in range(3))
+    same = passed_on(same, False)
+    cross = passed_on(cross, True)
+    summed = [one + two + three for one, two, three in arrived]
+    summed = summed[0] if len(summed) == 1 else jnp.concatenate(summed, axis=2)
+    regrouped = lax.all_to_all(summed, "mem", split_axis=0, concat_axis=0, tiled=True)
+    regrouped = regrouped.reshape(8 * groups, levels - turned, 128)
+    near_first = (rest + same + cross).reshape(8 * groups, turned, 128)
+    score = scored(0, near_first, observed)
+    copies = scored(turned, regrouped, observed, (score,), lax.axis_size("mem"))
     pieces = lax.all_to_all(copies, "mem", split_axis=0, concat_axis=0, tiled=True)
     return jnp.moveaxis(pieces, 0, 1).reshape(observed.shape)
 

time: 110 us -> 103 us (0.936)
  the two profiles are of different devices: /device:TPU:7 before, /device:TPU:6 now
where the time goes in v2:
time: 103 us
  starting transfers between devices  39.7 us (39%)
  waiting for transfers between devices  34.6 us (34%)
  blocking collectives  11.5 us (11%)
  Pallas kernels  9.89 us (10%)
  other arithmetic  4.42 us (4%)
  local copies, waits for them, and re-layouts  1.59 us (2%)
    ppermute x6, waiting for transfers between devices, passed_on(): return lax.ppermute(value, 'dom', pairs)  26.8 us
    ppermute x6, starting transfers between devices, passed_on(): return lax.ppermute(value, 'dom', pairs)  14 us
    all_to_all x1, blocking collectives, on_device(): lax.all_to_all(copies, 'mem', split_axis=0, concat_axis=0, tiled=True)  11.5 us
    all_to_all x1, starting transfers between devices, on_device(): lax.all_to_all(summed, 'mem', split_axis=0, concat_axis=0, tiled=True)  10.4 us
    all_to_all x1, starting transfers between devices, on_device(): mixed = lax.all_to_all(both, 'mem', split_axis=0, concat_axis=0, tiled=True)  10.3 us
    pallas_call x2, Pallas kernels, remap(): pl.pallas_call(functools.partial(remap_kernel, coded(table), parts, load)...  7.99 us
    all_to_all x1, waiting for transfers between devices, on_device(): lax.all_to_all(summed, 'mem', split_axis=0, concat_axis=0, tiled=True)  7.77 us
    ppermute x2, starting transfers between devices, swapped(): lax.ppermute(value, 'dom', [(source, source ^ 1) for source in range(coun...  4.97 us
  transfers between devices with their start and end apart: 10, of which 6 were waited for; matrix products, arithmetic and copies ran while one was open for 5% of the time, Pallas kernels for 4%

profile of v2, /device:TPU:6, one launch (start us, length us, event | category | flops | bytes accessed | tf_op | source)
XLA Modules:
  0.0 102.6 jit_solution(17613501559202463729)
XLA Ops:
  0.7 3.9 %shard_map.64 = (f32[1,8,6,32,128]{4,3,2,1,0:T(8,128)S(1)}, f32[2,8,6,32,128]{4,3,2,1,0:T(8,128)S(1)}, bf16[6,32,4096]{2,1,0:T(8,128)(2,1)S(1)}, bf16[96,128,128]{2,1,0:T(8,128)(2,1)S(1)}) custom-call(s32[96]{0:T(128)} %block_hbm.3, s32[96]{0:T(128)} %target_hbm.3, s32[1]{0:T(128)S(6)} %copy.16.count_hbm, bf16[6,32,4096]{2,1,0:T(8,128)(2,1)} %ens_in.1, ...), custom_call_target="tpu_custom_call" | custom-call | flops 603979776 | bytes 12000000 | tf_op jit(solution)/shard_map/pallas_call | solution.py:108
  4.5 2.2 %collective-permute-start.1 = (f32[2,8,6,32,128]{4,3,2,1,0:T(8,128)S(1)}, f32[2,8,6,32,128]{4,3,2,1,0:T(8,128)S(1)}, u32[]{:S(2)}, u32[]{:S(2)}) collective-permute-start(f32[2,8,6,32,128]{4,3,2,1,0:T(8,128)S(1)} %get-tuple-element.21), channel_id=1, source_target_pairs={{0,8},{8,0},{16,24},{24,16},{32,40},{40,32},{48,56},{56,48},{64,72... | collective-permute-start | bytes 4718600 | tf_op jit(solution)/shard_map/ppermute | solution.py:181
  6.7 4.1 %shard_map.65 = (f32[2,8,6,32,128]{4,3,2,1,0:T(8,128)S(1)}, f32[1,8,6,32,128]{4,3,2,1,0:T(8,128)S(1)}, f32[3,8,6,32,128]{4,3,2,1,0:T(8,128)S(1)}) custom-call(s32[96]{0:T(128)} %block_hbm.3, s32[96]{0:T(128)} %target_hbm.3, s32[1]{0:T(128)S(6)} %copy.16.count_hbm, bf16[6,32,4096]{2,1,0:T(8,128)(2,1)S(1)} %get-tuple-element.15.ens_in, ...), custom_call_target="tpu_custom_call" | custom-call | flops 603979776 | bytes 12000000 | tf_op jit(solution)/shard_map/pallas_call | solution.py:108
  10.8 2.8 %collective-permute-start = (f32[3,8,6,32,128]{4,3,2,1,0:T(8,128)S(1)}, f32[3,8,6,32,128]{4,3,2,1,0:T(8,128)S(1)}, u32[]{:S(2)}, u32[]{:S(2)}) collective-permute-start(f32[3,8,6,32,128]{4,3,2,1,0:T(8,128)S(1)} %get-tuple-element.18), channel_id=1, source_target_pairs={{0,8},{8,0},{16,24},{24,16},{32,40},{40,32},{48,56},{56,48},{64,72... | collective-permute-start | bytes 7077896 | tf_op jit(solution)/shard_map/ppermute | solution.py:181
  13.8 3.9 %collective-permute-start.3 = (f32[2,8,6,8,128]{4,3,2,1,0:T(8,128)S(1)}, f32[2,8,6,8,128]{4,3,2,1,0:T(8,128)S(1)}, u32[]{:S(2)}, u32[]{:S(2)}) collective-permute-start(f32[2,8,6,8,128]{4,3,2,1,0:T(8,128)S(1)} %pad_maximum_fusion.2), channel_id=1, source_target_pairs={{0,16},{16,32},{24,8},{32,48},{40,24},{48,64},{56,40},{64,80},{72,... | collective-permute-start | bytes 1179656 | tf_op jit(solution)/shard_map/ppermute | solution.py:192
  17.9 1.1 %pad_maximum_fusion = f32[2,8,6,24,128]{4,3,2,1,0:T(8,128)} fusion(f32[1,8,6,24,128]{4,3,2,1,0:T(8,128)S(1)} %get-tuple-element.32, f32[1,8,6,24,128]{4,3,2,1,0:T(8,128)S(1)} %get-tuple-element.31), kind=kLoop, calls=%fused_computation.1 | loop fusion | flops 294912 | bytes 2359296 | tf_op jit(solution)/shard_map/concatenate | solution.py:205
  19.0 2.4 %collective-permute-start.2 = (f32[2,8,6,24,128]{4,3,2,1,0:T(8,128)}, f32[2,8,6,24,128]{4,3,2,1,0:T(8,128)}, u32[]{:S(2)}, u32[]{:S(2)}) collective-permute-start(f32[2,8,6,24,128]{4,3,2,1,0:T(8,128)} %pad_maximum_fusion), channel_id=1, source_target_pairs={{0,16},{16,32},{24,8},{32,48},{40,24},{48,64},{56,40},{64,80},{72,... | collective-permute-start | bytes 3538952 | tf_op jit(solution)/shard_map/ppermute | solution.py:192
  22.0 3.5 %collective-permute-done.3 = f32[2,8,6,8,128]{4,3,2,1,0:T(8,128)S(1)} collective-permute-done((f32[2,8,6,8,128]{4,3,2,1,0:T(8,128)S(1)}, f32[2,8,6,8,128]{4,3,2,1,0:T(8,128)S(1)}, u32[]{:S(2)}, u32[]{:S(2)}) %collective-permute-start.3) | collective-permute-done | bytes 393248 | tf_op jit(solution)/shard_map/ppermute | solution.py:192
  25.7 0.9 copy.8
  26.6 10.3 %all-to-all-start.1 = ((f32[8,3,6,8,128]{4,3,2,1,0:T(8,128)}), f32[8,3,6,8,128]{4,3,2,1,0:T(8,128)S(1)}, u32[]{:S(2)}, u32[]{:S(2)}) async-start(f32[8,3,6,8,128]{4,3,2,1,0:T(8,128)} %copy.8), calls=%async_computation.1 | async-start | bytes 1179648 | tf_op jit(solution)/shard_map/all_to_all | solution.py:219
  36.9 2.7 %collective-permute-done.2 = f32[2,8,6,24,128]{4,3,2,1,0:T(8,128)} collective-permute-done((f32[2,8,6,24,128]{4,3,2,1,0:T(8,128)}, f32[2,8,6,24,128]{4,3,2,1,0:T(8,128)}, u32[]{:S(2)}, u32[]{:S(2)}) %collective-permute-start.2) | collective-permute-done | bytes 1179680 | tf_op jit(solution)/shard_map/ppermute | solution.py:192
  39.5 1.4 %add_bitcast_fusion = (f32[8,6,24,128]{3,2,1,0:T(8,128)S(1)}, f32[8,6,24,128]{3,2,1,0:T(8,128)S(1)}) fusion(f32[2,8,6,24,128]{4,3,2,1,0:T(8,128)} %collective-permute-done.2, f32[2,8,6,32,128]{4,3,2,1,0:T(8,128)S(1)} %slice_add_fusion), kind=kLoop, calls=%fused_computation.7 | loop fusion | flops 294912 | bytes 3538944 | tf_op jit(solution)/shard_map/add | solution.py:214
  40.9 1.9 %collective-permute-start.5 = (f32[8,6,24,128]{3,2,1,0:T(8,128)S(1)}, f32[8,6,24,128]{3,2,1,0:T(8,128)S(1)}, u32[]{:S(2)}, u32[]{:S(2)}) collective-permute-start(f32[8,6,24,128]{3,2,1,0:T(8,128)S(1)} %get-tuple-element.25), channel_id=1, source_target_pairs={{0,24},{16,40},{24,0},{32,56},{40,16},{48,72},{56,32},{64,88},{72,... | collective-permute-start | bytes 1769480 | tf_op jit(solution)/shard_map/ppermute | solution.py:192
  42.9 1.9 %collective-permute-start.4 = (f32[8,6,24,128]{3,2,1,0:T(8,128)S(1)}, f32[8,6,24,128]{3,2,1,0:T(8,128)S(1)}, u32[]{:S(2)}, u32[]{:S(2)}) collective-permute-start(f32[8,6,24,128]{3,2,1,0:T(8,128)S(1)} %get-tuple-element.26), channel_id=1, source_target_pairs={{0,16},{16,32},{24,8},{32,48},{40,24},{48,64},{56,40},{64,80},{72,... | collective-permute-start | bytes 1769480 | tf_op jit(solution)/shard_map/ppermute | solution.py:192
  44.8 7.3 %collective-permute-done.5 = f32[8,6,24,128]{3,2,1,0:T(8,128)S(1)} collective-permute-done((f32[8,6,24,128]{3,2,1,0:T(8,128)S(1)}, f32[8,6,24,128]{3,2,1,0:T(8,128)S(1)}, u32[]{:S(2)}, u32[]{:S(2)}) %collective-permute-start.5) | collective-permute-done | bytes 589856 | tf_op jit(solution)/shard_map/ppermute | solution.py:192
  52.1 7.5 %collective-permute-done.4 = f32[8,6,24,128]{3,2,1,0:T(8,128)S(1)} collective-permute-done((f32[8,6,24,128]{3,2,1,0:T(8,128)S(1)}, f32[8,6,24,128]{3,2,1,0:T(8,128)S(1)}, u32[]{:S(2)}, u32[]{:S(2)}) %collective-permute-start.4) | collective-permute-done | bytes 589856 | tf_op jit(solution)/shard_map/ppermute | solution.py:192
  59.6 0.9 slice_add_fusion.3
  60.6 10.4 %all-to-all-start = ((f32[8,6,24,128]{3,2,1,0:T(8,128)}), f32[8,6,24,128]{3,2,1,0:T(8,128)S(1)}, u32[]{:S(2)}, u32[]{:S(2)}) async-start(f32[8,6,24,128]{3,2,1,0:T(8,128)} %slice_add_fusion.3), calls=%async_computation | async-start | bytes 1179648 | tf_op jit(solution)/shard_map/all_to_all | solution.py:240
  71.0 1.9 %collective-permute-start.6 = (f32[8,6,8,128]{3,2,1,0:T(8,128)S(1)}, f32[8,6,8,128]{3,2,1,0:T(8,128)S(1)}, u32[]{:S(2)}, u32[]{:S(2)}) collective-permute-start(f32[8,6,8,128]{3,2,1,0:T(8,128)S(1)} %get-tuple-element.33), channel_id=1, source_target_pairs={{0,16},{16,32},{24,8},{32,48},{40,24},{48,64},{56,40},{64,80},{72,... | collective-permute-start | bytes 589832 | tf_op jit(solution)/shard_map/ppermute | solution.py:192
  73.0 1.9 %collective-permute-start.7 = (f32[8,6,8,128]{3,2,1,0:T(8,128)S(1)}, f32[8,6,8,128]{3,2,1,0:T(8,128)S(1)}, u32[]{:S(2)}, u32[]{:S(2)}) collective-permute-start(f32[8,6,8,128]{3,2,1,0:T(8,128)S(1)} %get-tuple-element.34), channel_id=1, source_target_pairs={{0,24},{16,40},{24,0},{32,56},{40,16},{48,72},{56,32},{64,88},{72,... | collective-permute-start | bytes 589832 | tf_op jit(solution)/shard_map/ppermute | solution.py:192
  74.9 5.8 %collective-permute-done.6 = f32[8,6,8,128]{3,2,1,0:T(8,128)S(1)} collective-permute-done((f32[8,6,8,128]{3,2,1,0:T(8,128)S(1)}, f32[8,6,8,128]{3,2,1,0:T(8,128)S(1)}, u32[]{:S(2)}, u32[]{:S(2)}) %collective-permute-start.6) | collective-permute-done | bytes 196640 | tf_op jit(solution)/shard_map/ppermute | solution.py:192
  81.2 7.8 %all-to-all-done = f32[8,6,24,128]{3,2,1,0:T(8,128)S(1)} async-done(((f32[8,6,24,128]{3,2,1,0:T(8,128)}), f32[8,6,24,128]{3,2,1,0:T(8,128)S(1)}, u32[]{:S(2)}, u32[]{:S(2)}) %all-to-all-start) | async-done | bytes 589856 | tf_op jit(solution)/shard_map/all_to_all | solution.py:240
  89.0 1.4 %shard_map.67 = f32[8,32,128]{2,1,0:T(8,128)S(1)} custom-call(f32[48,24,128]{2,1,0:T(8,128)S(1)} %bitcast.34, f32[32,1024]{1,0:T(8,128)S(1)} %copy-done, f32[8,128]{1,0:T(8,128)S(1)} %shard_map.66.rest_0_), custom_call_target="tpu_custom_call" | custom-call | flops 10616832 | bytes 589824 | tf_op jit(solution)/shard_map/pallas_call | solution.py:167
  90.4 11.5 %all_to_all.15 = f32[8,32,128]{2,1,0:T(8,128)S(1)} all-to-all(f32[8,32,128]{2,1,0:T(8,128)S(1)} %shard_map.67), channel_id=1, replica_groups=mesh['dom'=64,'mem'=8] {'mem'}, dimensions={0} | all-to-all | bytes 262144 | tf_op jit(solution)/shard_map/all_to_all | solution.py:245
  (18 shorter events, 2.2 us)
Async XLA Ops:
  4.5 9.1 %collective-permute-start.1 = (f32[2,8,6,32,128]{4,3,2,1,0:T(8,128)S(1)}, f32[2,8,6,32,128]{4,3,2,1,0:T(8,128)S(1)}, u32[]{:S(2)}, u32[]{:S(2)}) collective-permute-start(f32[2,8,6,32,128]{4,3,2,1,0:T(8,128)S(1)} %get-tuple-element.21), channel_id=1, source_target_pairs={{0,8},{8,0},{16,24},{24,16},{32,40},{40,32},{48,56},{56,48},{64,72... | collective-permute-start | bytes 4718600 | tf_op jit(solution)/shard_map/ppermute | solution.py:181
  10.8 10.6 %collective-permute-start = (f32[3,8,6,32,128]{4,3,2,1,0:T(8,128)S(1)}, f32[3,8,6,32,128]{4,3,2,1,0:T(8,128)S(1)}, u32[]{:S(2)}, u32[]{:S(2)}) collective-permute-start(f32[3,8,6,32,128]{4,3,2,1,0:T(8,128)S(1)} %get-tuple-element.18), channel_id=1, source_target_pairs={{0,8},{8,0},{16,24},{24,16},{32,40},{40,32},{48,56},{56,48},{64,72... | collective-permute-start | bytes 7077896 | tf_op jit(solution)/shard_map/ppermute | solution.py:181
  13.8 11.8 %collective-permute-start.3 = (f32[2,8,6,8,128]{4,3,2,1,0:T(8,128)S(1)}, f32[2,8,6,8,128]{4,3,2,1,0:T(8,128)S(1)}, u32[]{:S(2)}, u32[]{:S(2)}) collective-permute-start(f32[2,8,6,8,128]{4,3,2,1,0:T(8,128)S(1)} %pad_maximum_fusion.2), channel_id=1, source_target_pairs={{0,16},{16,32},{24,8},{32,48},{40,24},{48,64},{56,40},{64,80},{72,... | collective-permute-start | bytes 1179656 | tf_op jit(solution)/shard_map/ppermute | solution.py:192
  19.0 20.5 %collective-permute-start.2 = (f32[2,8,6,24,128]{4,3,2,1,0:T(8,128)}, f32[2,8,6,24,128]{4,3,2,1,0:T(8,128)}, u32[]{:S(2)}, u32[]{:S(2)}) collective-permute-start(f32[2,8,6,24,128]{4,3,2,1,0:T(8,128)} %pad_maximum_fusion), channel_id=1, source_target_pairs={{0,16},{16,32},{24,8},{32,48},{40,24},{48,64},{56,40},{64,80},{72,... | collective-permute-start | bytes 3538952 | tf_op jit(solution)/shard_map/ppermute | solution.py:192
  26.6 34.0 %all-to-all-start.1 = ((f32[8,3,6,8,128]{4,3,2,1,0:T(8,128)}), f32[8,3,6,8,128]{4,3,2,1,0:T(8,128)S(1)}, u32[]{:S(2)}, u32[]{:S(2)}) async-start(f32[8,3,6,8,128]{4,3,2,1,0:T(8,128)} %copy.8), calls=%async_computation.1 | async-start | bytes 1179648 | tf_op jit(solution)/shard_map/all_to_all | solution.py:219
  40.9 11.2 %collective-permute-start.5 = (f32[8,6,24,128]{3,2,1,0:T(8,128)S(1)}, f32[8,6,24,128]{3,2,1,0:T(8,128)S(1)}, u32[]{:S(2)}, u32[]{:S(2)}) collective-permute-start(f32[8,6,24,128]{3,2,1,0:T(8,128)S(1)} %get-tuple-element.25), channel_id=1, source_target_pairs={{0,24},{16,40},{24,0},{32,56},{40,16},{48,72},{56,32},{64,88},{72,... | collective-permute-start | bytes 1769480 | tf_op jit(solution)/shard_map/ppermute | solution.py:192
  42.9 16.8 %collective-permute-start.4 = (f32[8,6,24,128]{3,2,1,0:T(8,128)S(1)}, f32[8,6,24,128]{3,2,1,0:T(8,128)S(1)}, u32[]{:S(2)}, u32[]{:S(2)}) collective-permute-start(f32[8,6,24,128]{3,2,1,0:T(8,128)S(1)} %get-tuple-element.26), channel_id=1, source_target_pairs={{0,16},{16,32},{24,8},{32,48},{40,24},{48,64},{56,40},{64,80},{72,... | collective-permute-start | bytes 1769480 | tf_op jit(solution)/shard_map/ppermute | solution.py:192
  60.6 20.2 %copy-start = (f32[32,1024]{1,0:T(8,128)S(1)}, f32[32,1024]{1,0:T(8,128)}, u32[]{:S(2)}) copy-start(f32[32,1024]{1,0:T(8,128)} %observed_ref.3) | copy-start | bytes 393220
  60.6 28.5 %all-to-all-start = ((f32[8,6,24,128]{3,2,1,0:T(8,128)}), f32[8,6,24,128]{3,2,1,0:T(8,128)S(1)}, u32[]{:S(2)}, u32[]{:S(2)}) async-start(f32[8,6,24,128]{3,2,1,0:T(8,128)} %slice_add_fusion.3), calls=%async_computation | async-start | bytes 1179648 | tf_op jit(solution)/shard_map/all_to_all | solution.py:240
  71.0 9.7 %collective-permute-start.6 = (f32[8,6,8,128]{3,2,1,0:T(8,128)S(1)}, f32[8,6,8,128]{3,2,1,0:T(8,128)S(1)}, u32[]{:S(2)}, u32[]{:S(2)}) collective-permute-start(f32[8,6,8,128]{3,2,1,0:T(8,128)S(1)} %get-tuple-element.33), channel_id=1, source_target_pairs={{0,16},{16,32},{24,8},{32,48},{40,24},{48,64},{56,40},{64,80},{72,... | collective-permute-start | bytes 589832 | tf_op jit(solution)/shard_map/ppermute | solution.py:192
  73.0 7.7 %collective-permute-start.7 = (f32[8,6,8,128]{3,2,1,0:T(8,128)S(1)}, f32[8,6,8,128]{3,2,1,0:T(8,128)S(1)}, u32[]{:S(2)}, u32[]{:S(2)}) collective-permute-start(f32[8,6,8,128]{3,2,1,0:T(8,128)S(1)} %get-tuple-element.34), channel_id=1, source_target_pairs={{0,24},{16,40},{24,0},{32,56},{40,16},{48,72},{56,32},{64,88},{72,... | collective-permute-start | bytes 589832 | tf_op jit(solution)/shard_map/ppermute | solution.py:192

commit v3 on v1

--- a/solution.py
+++ b/solution.py
@@ -8,7 +8,7 @@
 from jax.sharding import PartitionSpec as P
 
 
-CHUNKS = (16, 16)
+CHUNKS = (8, 24)
 
 FAR = {4: 0, -3: 1, -4: 2}
 NEAR = {2: 0, 3: 1, 0: 2, -1: 3, -2: 4, 1: 5}
@@ -62,11 +62,15 @@
         slots[found] = slot * 256 + code * owned + (target & 7)
         return found + jnp.where((code < 7) & (slot < live), 1, 0)
 
-    found = lax.fori_loop(0, total, listed, jnp.int32(0), unroll=8)
+    pieces = 4
+    span = total // pieces
+    found = jnp.int32(0)
+    ends = []
+    for piece in range(pieces):
+        found = lax.fori_loop(piece * span, (piece + 1) * span, listed, found, unroll=8)
+        ends.append(found)
     for extra in range(UNROLL):
         slots[found + extra] = dump
-    for copy in large:
-        copy.wait()
 
     def added(step, carry):
         results = []
@@ -82,7 +86,17 @@
             acc[tile] += result
         return carry
 
-    lax.fori_loop(0, (found + UNROLL - 1) // UNROLL, added, 0)
+    steps = [end // UNROLL for end in ends[:-1]] + [(found + UNROLL - 1) // UNROLL]
+    if load:
+        for copy in large[:groups]:
+            copy.wait()
+        begin = 0
+        for copy, step in zip(large[groups:], steps):
+            copy.wait()
+            lax.fori_loop(begin, step, added, 0)
+            begin = step
+    else:
+        lax.fori_loop(0, steps[-1], added, 0)
 
     def stored(tile, carry):
         part = 0
@@ -125,6 +139,21 @@
     )(tile_block, tile_target, tile_count, ensemble, tile_weight)
 
 
+def comparators(count):
+    found = []
+    half = 1
+    while half < count:
+        step = half
+        while step >= 1:
+            for start in range(step % half, count - step, 2 * step):
+                for place in range(start, min(start + step, count - step)):
+                    if place // (2 * half) == (place + step) // (2 * half):
+                        found.append((place, place + step))
+            step //= 2
+        half *= 2
+    return found
+
+
 def score_kernel(first, copies, members_ref, observed_ref, *rest):
     before, out = rest[:-1], rest[-1]
     members, length, cells = members_ref.shape
@@ -139,14 +168,16 @@
         skill = jnp.zeros((8, cells), jnp.float32)
         spread = jnp.zeros((8, cells), jnp.float32)
         values = [members_ref[member, pl.ds(low, 8)] for member in range(members)]
-        for left in range(members):
-            skill = skill + jnp.abs(values[left] - observed)
-            row = None
-            for right in range(left + 1, members):
-                gap = jnp.abs(values[left] - values[right])
-                row = gap if row is None else row + gap
-            if row is not None:
-                spread = spread + row
+        for value in values:
+            skill = skill + jnp.abs(value - observed)
+        for under, over in comparators(members):
+            values[under], values[over] = (
+                jnp.minimum(values[under], values[over]),
+                jnp.maximum(values[under], values[over]),
+            )
+        for below in range(members - 1):
+            pairs = float((below + 1) * (members - 1 - below))
+            spread = spread + pairs * (values[below + 1] - values[below])
         scores.append((done + low, skill / members - spread / (members * (members - 1.0))))
     if copies:
         for start, score in scores:

time: 110 us -> 119 us (1.082)
  the two profiles are of different devices: /device:TPU:7 before, /device:TPU:6 now
where the time goes in v3:
time: 119 us; the launch traced here: 118 us
  waiting for transfers between devices  57.1 us (48%)
  starting transfers between devices  37.2 us (31%)
  blocking collectives  11.9 us (10%)
  Pallas kernels  7.93 us (7%)
  other arithmetic  2.65 us (2%)
    all_to_all x2, waiting for transfers between devices, on_device(): lax.all_to_all(summed, 'mem', split_axis=0, concat_axis=0, tiled=True)  29.7 us
    ppermute x6, waiting for transfers between devices, passed_on(): return lax.ppermute(value, 'dom', pairs)  27.5 us
    ppermute x6, starting transfers between devices, passed_on(): return lax.ppermute(value, 'dom', pairs)  18.3 us
    all_to_all x2, starting transfers between devices, on_device(): lax.all_to_all(summed, 'mem', split_axis=0, concat_axis=0, tiled=True)  13.9 us
    all_to_all x1, blocking collectives, on_device(): lax.all_to_all(copies, 'mem', split_axis=0, concat_axis=0, tiled=True)  11.9 us
    pallas_call x2, Pallas kernels, remap(): pl.pallas_call(functools.partial(remap_kernel, coded(table), parts, load)...  7.3 us
    ppermute x2, starting transfers between devices, swapped(): lax.ppermute(value, 'dom', [(source, source ^ 1) for source in range(coun...  4.97 us
  transfers between devices with their start and end apart: 10, of which 4 were waited for; matrix products, arithmetic and copies ran while one was open for 2% of the time, Pallas kernels for 4%

profile of v3, /device:TPU:6, one launch (start us, length us, event | category | flops | bytes accessed | tf_op | source)
XLA Modules:
  0.0 118.3 jit_solution(17374353704342724635)
XLA Ops:
  0.7 3.2 %shard_map.64 = (f32[1,8,6,32,128]{4,3,2,1,0:T(8,128)S(1)}, f32[2,8,6,32,128]{4,3,2,1,0:T(8,128)S(1)}, bf16[6,32,4096]{2,1,0:T(8,128)(2,1)S(1)}, bf16[96,128,128]{2,1,0:T(8,128)(2,1)S(1)}) custom-call(s32[96]{0:T(128)} %block_hbm.3, s32[96]{0:T(128)} %target_hbm.3, s32[1]{0:T(128)S(6)} %copy.10.count_hbm, bf16[6,32,4096]{2,1,0:T(8,128)(2,1)} %ens_in.1, ...), custom_call_target="tpu_custom_call" | custom-call | flops 603979776 | bytes 12000000 | tf_op jit(solution)/shard_map/pallas_call | solution.py:122
  3.9 2.2 %collective-permute-start.1 = (f32[2,8,6,32,128]{4,3,2,1,0:T(8,128)S(1)}, f32[2,8,6,32,128]{4,3,2,1,0:T(8,128)S(1)}, u32[]{:S(2)}, u32[]{:S(2)}) collective-permute-start(f32[2,8,6,32,128]{4,3,2,1,0:T(8,128)S(1)} %get-tuple-element.20), channel_id=1, source_target_pairs={{0,8},{8,0},{16,24},{24,16},{32,40},{40,32},{48,56},{56,48},{64,72... | collective-permute-start | bytes 4718600 | tf_op jit(solution)/shard_map/ppermute | solution.py:212
  6.0 4.1 %shard_map.65 = (f32[2,8,6,32,128]{4,3,2,1,0:T(8,128)S(1)}, f32[1,8,6,32,128]{4,3,2,1,0:T(8,128)S(1)}, f32[3,8,6,32,128]{4,3,2,1,0:T(8,128)S(1)}) custom-call(s32[96]{0:T(128)} %block_hbm.3, s32[96]{0:T(128)} %target_hbm.3, s32[1]{0:T(128)S(6)} %copy.10.count_hbm, bf16[6,32,4096]{2,1,0:T(8,128)(2,1)S(1)} %get-tuple-element.15.ens_in, ...), custom_call_target="tpu_custom_call" | custom-call | flops 603979776 | bytes 12000000 | tf_op jit(solution)/shard_map/pallas_call | solution.py:122
  10.1 2.8 %collective-permute-start = (f32[3,8,6,32,128]{4,3,2,1,0:T(8,128)S(1)}, f32[3,8,6,32,128]{4,3,2,1,0:T(8,128)S(1)}, u32[]{:S(2)}, u32[]{:S(2)}) collective-permute-start(f32[3,8,6,32,128]{4,3,2,1,0:T(8,128)S(1)} %get-tuple-element.18), channel_id=1, source_target_pairs={{0,8},{8,0},{16,24},{24,16},{32,40},{40,32},{48,56},{56,48},{64,72... | collective-permute-start | bytes 7077896 | tf_op jit(solution)/shard_map/ppermute | solution.py:212
  13.0 0.2 slice_add_fusion.2
  13.2 3.9 %collective-permute-start.2 = (f32[2,8,6,24,128]{4,3,2,1,0:T(8,128)S(1)}, f32[2,8,6,24,128]{4,3,2,1,0:T(8,128)S(1)}, u32[]{:S(2)}, u32[]{:S(2)}) collective-permute-start(f32[2,8,6,24,128]{4,3,2,1,0:T(8,128)S(1)} %pad_maximum_fusion), channel_id=1, source_target_pairs={{0,16},{16,32},{24,8},{32,48},{40,24},{48,64},{56,40},{64,80},{72,... | collective-permute-start | bytes 3538952 | tf_op jit(solution)/shard_map/ppermute | solution.py:223
  17.3 2.4 %collective-permute-start.3 = (f32[2,8,6,8,128]{4,3,2,1,0:T(8,128)S(1)}, f32[2,8,6,8,128]{4,3,2,1,0:T(8,128)S(1)}, u32[]{:S(2)}, u32[]{:S(2)}) collective-permute-start(f32[2,8,6,8,128]{4,3,2,1,0:T(8,128)S(1)} %pad_maximum_fusion.1), channel_id=1, source_target_pairs={{0,16},{16,32},{24,8},{32,48},{40,24},{48,64},{56,40},{64,80},{72,... | collective-permute-start | bytes 1179656 | tf_op jit(solution)/shard_map/ppermute | solution.py:223
  19.7 18.0 %collective-permute-done.3 = f32[2,8,6,8,128]{4,3,2,1,0:T(8,128)S(1)} collective-permute-done((f32[2,8,6,8,128]{4,3,2,1,0:T(8,128)S(1)}, f32[2,8,6,8,128]{4,3,2,1,0:T(8,128)S(1)}, u32[]{:S(2)}, u32[]{:S(2)}) %collective-permute-start.3) | collective-permute-done | bytes 393248 | tf_op jit(solution)/shard_map/ppermute | solution.py:223
  37.8 0.3 fusion.2
  38.1 1.9 %collective-permute-start.5 = (f32[8,6,24,128]{3,2,1,0:T(8,128)S(1)}, f32[8,6,24,128]{3,2,1,0:T(8,128)S(1)}, u32[]{:S(2)}, u32[]{:S(2)}) collective-permute-start(f32[8,6,24,128]{3,2,1,0:T(8,128)S(1)} %get-tuple-element.25), channel_id=1, source_target_pairs={{0,24},{16,40},{24,0},{32,56},{40,16},{48,72},{56,32},{64,88},{72,... | collective-permute-start | bytes 1769480 | tf_op jit(solution)/shard_map/ppermute | solution.py:223
  40.1 1.9 %collective-permute-start.4 = (f32[8,6,24,128]{3,2,1,0:T(8,128)S(1)}, f32[8,6,24,128]{3,2,1,0:T(8,128)S(1)}, u32[]{:S(2)}, u32[]{:S(2)}) collective-permute-start(f32[8,6,24,128]{3,2,1,0:T(8,128)S(1)} %get-tuple-element.26), channel_id=1, source_target_pairs={{0,16},{16,32},{24,8},{32,48},{40,24},{48,64},{56,40},{64,80},{72,... | collective-permute-start | bytes 1769480 | tf_op jit(solution)/shard_map/ppermute | solution.py:223
  42.0 4.6 %collective-permute-start.6 = (f32[8,6,8,128]{3,2,1,0:T(8,128)S(1)}, f32[8,6,8,128]{3,2,1,0:T(8,128)S(1)}, u32[]{:S(2)}, u32[]{:S(2)}) collective-permute-start(f32[8,6,8,128]{3,2,1,0:T(8,128)S(1)} %get-tuple-element.28), channel_id=1, source_target_pairs={{0,16},{16,32},{24,8},{32,48},{40,24},{48,64},{56,40},{64,80},{72,... | collective-permute-start | bytes 589832 | tf_op jit(solution)/shard_map/ppermute | solution.py:223
  46.6 3.6 %collective-permute-start.7 = (f32[8,6,8,128]{3,2,1,0:T(8,128)S(1)}, f32[8,6,8,128]{3,2,1,0:T(8,128)S(1)}, u32[]{:S(2)}, u32[]{:S(2)}) collective-permute-start(f32[8,6,8,128]{3,2,1,0:T(8,128)S(1)} %get-tuple-element.27), channel_id=1, source_target_pairs={{0,24},{16,40},{24,0},{32,56},{40,16},{48,72},{56,32},{64,88},{72,... | collective-permute-start | bytes 589832 | tf_op jit(solution)/shard_map/ppermute | solution.py:223
  50.4 9.5 %collective-permute-done.7 = f32[8,6,8,128]{3,2,1,0:T(8,128)S(1)} collective-permute-done((f32[8,6,8,128]{3,2,1,0:T(8,128)S(1)}, f32[8,6,8,128]{3,2,1,0:T(8,128)S(1)}, u32[]{:S(2)}, u32[]{:S(2)}) %collective-permute-start.7) | collective-permute-done | bytes 196640 | tf_op jit(solution)/shard_map/ppermute | solution.py:223
  59.9 0.7 fusion.7
  60.6 10.3 %all-to-all-start.1 = ((f32[8,6,8,128]{3,2,1,0:T(8,128)}), f32[8,6,8,128]{3,2,1,0:T(8,128)S(1)}, u32[]{:S(2)}, u32[]{:S(2)}) async-start(f32[8,6,8,128]{3,2,1,0:T(8,128)} %fusion.7), calls=%async_computation.1 | async-start | bytes 393216 | tf_op jit(solution)/shard_map/all_to_all | solution.py:265
  71.0 0.9 fusion.5
  71.9 10.5 %all-to-all-done.1 = f32[8,6,8,128]{3,2,1,0:T(8,128)S(1)} async-done(((f32[8,6,8,128]{3,2,1,0:T(8,128)}), f32[8,6,8,128]{3,2,1,0:T(8,128)S(1)}, u32[]{:S(2)}, u32[]{:S(2)}) %all-to-all-start.1) | async-done | bytes 196640 | tf_op jit(solution)/shard_map/all_to_all | solution.py:265
  82.4 3.5 %all-to-all-start = ((f32[8,6,24,128]{3,2,1,0:T(8,128)}), f32[8,6,24,128]{3,2,1,0:T(8,128)S(1)}, u32[]{:S(2)}, u32[]{:S(2)}) async-start(f32[8,6,24,128]{3,2,1,0:T(8,128)} %fusion.5), calls=%async_computation | async-start | bytes 1179648 | tf_op jit(solution)/shard_map/all_to_all | solution.py:265
  85.9 0.2 shard_map.66.rest_0_
  86.1 19.2 %all-to-all-done = f32[8,6,24,128]{3,2,1,0:T(8,128)S(1)} async-done(((f32[8,6,24,128]{3,2,1,0:T(8,128)}), f32[8,6,24,128]{3,2,1,0:T(8,128)S(1)}, u32[]{:S(2)}, u32[]{:S(2)}) %all-to-all-start) | async-done | bytes 589856 | tf_op jit(solution)/shard_map/all_to_all | solution.py:265
  105.3 0.5 shard_map.67
  105.7 11.9 %all_to_all.15 = f32[8,32,128]{2,1,0:T(8,128)S(1)} all-to-all(f32[8,32,128]{2,1,0:T(8,128)S(1)} %shard_map.67), channel_id=1, replica_groups=mesh['dom'=64,'mem'=8] {'mem'}, dimensions={0} | all-to-all | bytes 262144 | tf_op jit(solution)/shard_map/all_to_all | solution.py:272
  117.6 0.7 copy_bitcast_fusion
  (13 shorter events, 0.5 us)
Async XLA Ops:
  3.9 9.1 %collective-permute-start.1 = (f32[2,8,6,32,128]{4,3,2,1,0:T(8,128)S(1)}, f32[2,8,6,32,128]{4,3,2,1,0:T(8,128)S(1)}, u32[]{:S(2)}, u32[]{:S(2)}) collective-permute-start(f32[2,8,6,32,128]{4,3,2,1,0:T(8,128)S(1)} %get-tuple-element.20), channel_id=1, source_target_pairs={{0,8},{8,0},{16,24},{24,16},{32,40},{40,32},{48,56},{56,48},{64,72... | collective-permute-start | bytes 4718600 | tf_op jit(solution)/shard_map/ppermute | solution.py:212
  10.1 27.5 %collective-permute-start = (f32[3,8,6,32,128]{4,3,2,1,0:T(8,128)S(1)}, f32[3,8,6,32,128]{4,3,2,1,0:T(8,128)S(1)}, u32[]{:S(2)}, u32[]{:S(2)}) collective-permute-start(f32[3,8,6,32,128]{4,3,2,1,0:T(8,128)S(1)} %get-tuple-element.18), channel_id=1, source_target_pairs={{0,8},{8,0},{16,24},{24,16},{32,40},{40,32},{48,56},{56,48},{64,72... | collective-permute-start | bytes 7077896 | tf_op jit(solution)/shard_map/ppermute | solution.py:212
  13.2 24.6 %collective-permute-start.2 = (f32[2,8,6,24,128]{4,3,2,1,0:T(8,128)S(1)}, f32[2,8,6,24,128]{4,3,2,1,0:T(8,128)S(1)}, u32[]{:S(2)}, u32[]{:S(2)}) collective-permute-start(f32[2,8,6,24,128]{4,3,2,1,0:T(8,128)S(1)} %pad_maximum_fusion), channel_id=1, source_target_pairs={{0,16},{16,32},{24,8},{32,48},{40,24},{48,64},{56,40},{64,80},{72,... | collective-permute-start | bytes 3538952 | tf_op jit(solution)/shard_map/ppermute | solution.py:223
  17.3 20.4 %collective-permute-start.3 = (f32[2,8,6,8,128]{4,3,2,1,0:T(8,128)S(1)}, f32[2,8,6,8,128]{4,3,2,1,0:T(8,128)S(1)}, u32[]{:S(2)}, u32[]{:S(2)}) collective-permute-start(f32[2,8,6,8,128]{4,3,2,1,0:T(8,128)S(1)} %pad_maximum_fusion.1), channel_id=1, source_target_pairs={{0,16},{16,32},{24,8},{32,48},{40,24},{48,64},{56,40},{64,80},{72,... | collective-permute-start | bytes 1179656 | tf_op jit(solution)/shard_map/ppermute | solution.py:223
  38.1 32.8 %collective-permute-start.5 = (f32[8,6,24,128]{3,2,1,0:T(8,128)S(1)}, f32[8,6,24,128]{3,2,1,0:T(8,128)S(1)}, u32[]{:S(2)}, u32[]{:S(2)}) collective-permute-start(f32[8,6,24,128]{3,2,1,0:T(8,128)S(1)} %get-tuple-element.25), channel_id=1, source_target_pairs={{0,24},{16,40},{24,0},{32,56},{40,16},{48,72},{56,32},{64,88},{72,... | collective-permute-start | bytes 1769480 | tf_op jit(solution)/shard_map/ppermute | solution.py:223
  40.1 30.9 %collective-permute-start.4 = (f32[8,6,24,128]{3,2,1,0:T(8,128)S(1)}, f32[8,6,24,128]{3,2,1,0:T(8,128)S(1)}, u32[]{:S(2)}, u32[]{:S(2)}) collective-permute-start(f32[8,6,24,128]{3,2,1,0:T(8,128)S(1)} %get-tuple-element.26), channel_id=1, source_target_pairs={{0,16},{16,32},{24,8},{32,48},{40,24},{48,64},{56,40},{64,80},{72,... | collective-permute-start | bytes 1769480 | tf_op jit(solution)/shard_map/ppermute | solution.py:223
  42.0 17.9 %collective-permute-start.6 = (f32[8,6,8,128]{3,2,1,0:T(8,128)S(1)}, f32[8,6,8,128]{3,2,1,0:T(8,128)S(1)}, u32[]{:S(2)}, u32[]{:S(2)}) collective-permute-start(f32[8,6,8,128]{3,2,1,0:T(8,128)S(1)} %get-tuple-element.28), channel_id=1, source_target_pairs={{0,16},{16,32},{24,8},{32,48},{40,24},{48,64},{56,40},{64,80},{72,... | collective-permute-start | bytes 589832 | tf_op jit(solution)/shard_map/ppermute | solution.py:223
  46.6 13.3 %collective-permute-start.7 = (f32[8,6,8,128]{3,2,1,0:T(8,128)S(1)}, f32[8,6,8,128]{3,2,1,0:T(8,128)S(1)}, u32[]{:S(2)}, u32[]{:S(2)}) collective-permute-start(f32[8,6,8,128]{3,2,1,0:T(8,128)S(1)} %get-tuple-element.27), channel_id=1, source_target_pairs={{0,24},{16,40},{24,0},{32,56},{40,16},{48,72},{56,32},{64,88},{72,... | collective-permute-start | bytes 589832 | tf_op jit(solution)/shard_map/ppermute | solution.py:223
  60.6 21.8 %all-to-all-start.1 = ((f32[8,6,8,128]{3,2,1,0:T(8,128)}), f32[8,6,8,128]{3,2,1,0:T(8,128)S(1)}, u32[]{:S(2)}, u32[]{:S(2)}) async-start(f32[8,6,8,128]{3,2,1,0:T(8,128)} %fusion.7), calls=%async_computation.1 | async-start | bytes 393216 | tf_op jit(solution)/shard_map/all_to_all | solution.py:265
  70.9 15.0 %copy-start = (f32[32,1024]{1,0:T(8,128)S(1)}, f32[32,1024]{1,0:T(8,128)}, u32[]{:S(2)}) copy-start(f32[32,1024]{1,0:T(8,128)} %observed_ref.3) | copy-start | bytes 393220
  82.4 22.9 %all-to-all-start = ((f32[8,6,24,128]{3,2,1,0:T(8,128)}), f32[8,6,24,128]{3,2,1,0:T(8,128)S(1)}, u32[]{:S(2)}, u32[]{:S(2)}) async-start(f32[8,6,24,128]{3,2,1,0:T(8,128)} %fusion.5), calls=%async_computation | async-start | bytes 1179648 | tf_op jit(solution)/shard_map/all_to_all | solution.py:265

commit v4 on v3

--- a/solution.py
+++ b/solution.py
@@ -8,7 +8,8 @@
 from jax.sharding import PartitionSpec as P
 
 
-CHUNKS = (8, 24)
+CHUNKS = (16, 16)
+MIXES = ((0, 1),)
 
 FAR = {4: 0, -3: 1, -4: 2}
 NEAR = {2: 0, 3: 1, 0: 2, -1: 3, -2: 4, 1: 5}
@@ -256,19 +257,26 @@
         first += length
     scores = []
     first = 0
-    for index, length in enumerate(CHUNKS):
-        part = slice(first, first + length)
-        arrived = hops[index]
-        if index:
-            arrived, before = lax.optimization_barrier((arrived, summed))
-        summed = here[:, :, part] + arrived[0] + arrived[1]
-        regrouped = lax.all_to_all(summed, "mem", split_axis=0, concat_axis=0, tiled=True)
-        regrouped = regrouped.reshape(8 * groups, length, 128)
-        if index + 1 < len(CHUNKS):
-            scores.append(scored(first, regrouped, observed))
+    summed = None
+    for mix, members in enumerate(MIXES):
+        begin = first
+        totals = []
+        for index in members:
+            part = slice(first, first + CHUNKS[index])
+            arrived = hops[index]
+            if summed is not None:
+                arrived, before = lax.optimization_barrier((arrived, summed))
+            summed = here[:, :, part] + arrived[0] + arrived[1]
+            totals.append(summed)
+            first += CHUNKS[index]
+        if len(totals) > 1:
+            totals = [jnp.concatenate(totals, axis=2)]
+        regrouped = lax.all_to_all(totals[0], "mem", split_axis=0, concat_axis=0, tiled=True)
+        regrouped = regrouped.reshape(8 * groups, first - begin, 128)
+        if mix + 1 < len(MIXES):
+            scores.append(scored(begin, regrouped, observed))
         else:
-            copies = scored(first, regrouped, observed, scores, lax.axis_size("mem"))
-        first += length
+            copies = scored(begin, regrouped, observed, scores, lax.axis_size("mem"))
     pieces = lax.all_to_all(copies, "mem", split_axis=0, concat_axis=0, tiled=True)
     return jnp.moveaxis(pieces, 0, 1).reshape(observed.shape)
 

time: 119 us -> 101 us (0.85)
  the two profiles are of different devices: /device:TPU:6 before, /device:TPU:35 now
where the time goes in v4:
time: 101 us; the launch traced here: 100 us
  blocking collectives  44.4 us (44%)
  starting transfers between devices  26.2 us (26%)
  waiting for transfers between devices  17.6 us (17%)
  Pallas kernels  9.19 us (9%)
  other arithmetic  1.26 us (1%)
    all_to_all x1, blocking collectives, on_device(): lax.all_to_all(totals[0], 'mem', split_axis=0, concat_axis=0, tiled=True)  32.5 us
    ppermute x6, starting transfers between devices, passed_on(): return lax.ppermute(value, 'dom', pairs)  21.7 us
    ppermute x6, waiting for transfers between devices, passed_on(): return lax.ppermute(value, 'dom', pairs)  17.6 us
    all_to_all x1, blocking collectives, on_device(): lax.all_to_all(copies, 'mem', split_axis=0, concat_axis=0, tiled=True)  12 us
    pallas_call x2, Pallas kernels, remap(): pl.pallas_call(functools.partial(remap_kernel, coded(table), parts, load)...  8.59 us
    ppermute x2, starting transfers between devices, swapped(): lax.ppermute(value, 'dom', [(source, source ^ 1) for source in range(coun...  4.52 us
  transfers between devices with their start and end apart: 8, of which 4 were waited for; matrix products, arithmetic and copies ran while one was open for 1% of the time, Pallas kernels for 5%

profile of v4, /device:TPU:35, one launch (start us, length us, event | category | flops | bytes accessed | tf_op | source)
XLA Modules:
  0.0 100.2 jit_solution(8565977443379611449)
XLA Ops:
  0.7 3.8 %shard_map.64 = (f32[1,8,6,32,128]{4,3,2,1,0:T(8,128)S(1)}, f32[2,8,6,32,128]{4,3,2,1,0:T(8,128)S(1)}, bf16[6,32,4096]{2,1,0:T(8,128)(2,1)S(1)}, bf16[96,128,128]{2,1,0:T(8,128)(2,1)S(1)}) custom-call(s32[96]{0:T(128)} %block_hbm.3, s32[96]{0:T(128)} %target_hbm.3, s32[1]{0:T(128)S(6)} %copy.10.count_hbm, bf16[6,32,4096]{2,1,0:T(8,128)(2,1)} %ens_in.1, ...), custom_call_target="tpu_custom_call" | custom-call | flops 603979776 | bytes 12000000 | tf_op jit(solution)/shard_map/pallas_call | solution.py:123
  4.5 2.6 %collective-permute-start.1 = (f32[2,8,6,32,128]{4,3,2,1,0:T(8,128)S(1)}, f32[2,8,6,32,128]{4,3,2,1,0:T(8,128)S(1)}, u32[]{:S(2)}, u32[]{:S(2)}) collective-permute-start(f32[2,8,6,32,128]{4,3,2,1,0:T(8,128)S(1)} %get-tuple-element.20), channel_id=1, source_target_pairs={{0,8},{8,0},{16,24},{24,16},{32,40},{40,32},{48,56},{56,48},{64,72... | collective-permute-start | bytes 4718600 | tf_op jit(solution)/shard_map/ppermute | solution.py:213
  7.1 4.8 %shard_map.65 = (f32[2,8,6,32,128]{4,3,2,1,0:T(8,128)S(1)}, f32[1,8,6,32,128]{4,3,2,1,0:T(8,128)S(1)}, f32[3,8,6,32,128]{4,3,2,1,0:T(8,128)S(1)}) custom-call(s32[96]{0:T(128)} %block_hbm.3, s32[96]{0:T(128)} %target_hbm.3, s32[1]{0:T(128)S(6)} %copy.10.count_hbm, bf16[6,32,4096]{2,1,0:T(8,128)(2,1)S(1)} %get-tuple-element.15.ens_in, ...), custom_call_target="tpu_custom_call" | custom-call | flops 603979776 | bytes 12000000 | tf_op jit(solution)/shard_map/pallas_call | solution.py:123
  11.9 1.9 %collective-permute-start = (f32[3,8,6,32,128]{4,3,2,1,0:T(8,128)S(1)}, f32[3,8,6,32,128]{4,3,2,1,0:T(8,128)S(1)}, u32[]{:S(2)}, u32[]{:S(2)}) collective-permute-start(f32[3,8,6,32,128]{4,3,2,1,0:T(8,128)S(1)} %get-tuple-element.18), channel_id=1, source_target_pairs={{0,8},{8,0},{16,24},{24,16},{32,40},{40,32},{48,56},{56,48},{64,72... | collective-permute-start | bytes 7077896 | tf_op jit(solution)/shard_map/ppermute | solution.py:213
  13.8 0.2 slice_add_fusion.8
  14.1 1.9 %collective-permute-start.2 = (f32[2,8,6,16,128]{4,3,2,1,0:T(8,128)S(1)}, f32[2,8,6,16,128]{4,3,2,1,0:T(8,128)S(1)}, u32[]{:S(2)}, u32[]{:S(2)}) collective-permute-start(f32[2,8,6,16,128]{4,3,2,1,0:T(8,128)S(1)} %pad_maximum_fusion), channel_id=1, source_target_pairs={{0,16},{16,32},{24,8},{32,48},{40,24},{48,64},{56,40},{64,80},{72,... | collective-permute-start | bytes 2359304 | tf_op jit(solution)/shard_map/ppermute | solution.py:224
  16.1 2.4 %collective-permute-start.5 = (f32[2,8,6,16,128]{4,3,2,1,0:T(8,128)S(1)}, f32[2,8,6,16,128]{4,3,2,1,0:T(8,128)S(1)}, u32[]{:S(2)}, u32[]{:S(2)}) collective-permute-start(f32[2,8,6,16,128]{4,3,2,1,0:T(8,128)S(1)} %pad_maximum_fusion.1), channel_id=1, source_target_pairs={{0,16},{16,32},{24,8},{32,48},{40,24},{48,64},{56,40},{64,80},{72,... | collective-permute-start | bytes 2359304 | tf_op jit(solution)/shard_map/ppermute | solution.py:224
  18.5 8.6 %collective-permute-done.2 = f32[2,8,6,16,128]{4,3,2,1,0:T(8,128)S(1)} collective-permute-done((f32[2,8,6,16,128]{4,3,2,1,0:T(8,128)S(1)}, f32[2,8,6,16,128]{4,3,2,1,0:T(8,128)S(1)}, u32[]{:S(2)}, u32[]{:S(2)}) %collective-permute-start.2) | collective-permute-done | bytes 786464 | tf_op jit(solution)/shard_map/ppermute | solution.py:224
  27.2 0.2 fusion.6
  27.4 2.8 %collective-permute-start.3 = (f32[8,6,16,128]{3,2,1,0:T(8,128)S(1)}, f32[8,6,16,128]{3,2,1,0:T(8,128)S(1)}, u32[]{:S(2)}, u32[]{:S(2)}) collective-permute-start(f32[8,6,16,128]{3,2,1,0:T(8,128)S(1)} %get-tuple-element.26), channel_id=1, source_target_pairs={{0,16},{16,32},{24,8},{32,48},{40,24},{48,64},{56,40},{64,80},{72,... | collective-permute-start | bytes 1179656 | tf_op jit(solution)/shard_map/ppermute | solution.py:224
  30.2 6.4 %collective-permute-start.4 = (f32[8,6,16,128]{3,2,1,0:T(8,128)S(1)}, f32[8,6,16,128]{3,2,1,0:T(8,128)S(1)}, u32[]{:S(2)}, u32[]{:S(2)}) collective-permute-start(f32[8,6,16,128]{3,2,1,0:T(8,128)S(1)} %get-tuple-element.25), channel_id=1, source_target_pairs={{0,24},{16,40},{24,0},{32,56},{40,16},{48,72},{56,32},{64,88},{72,... | collective-permute-start | bytes 1179656 | tf_op jit(solution)/shard_map/ppermute | solution.py:224
  36.6 0.2 fusion.2
  36.9 1.9 %collective-permute-start.6 = (f32[8,6,16,128]{3,2,1,0:T(8,128)S(1)}, f32[8,6,16,128]{3,2,1,0:T(8,128)S(1)}, u32[]{:S(2)}, u32[]{:S(2)}) collective-permute-start(f32[8,6,16,128]{3,2,1,0:T(8,128)S(1)} %get-tuple-element.28), channel_id=1, source_target_pairs={{0,16},{16,32},{24,8},{32,48},{40,24},{48,64},{56,40},{64,80},{72,... | collective-permute-start | bytes 1179656 | tf_op jit(solution)/shard_map/ppermute | solution.py:224
  38.8 6.2 %collective-permute-start.7 = (f32[8,6,16,128]{3,2,1,0:T(8,128)S(1)}, f32[8,6,16,128]{3,2,1,0:T(8,128)S(1)}, u32[]{:S(2)}, u32[]{:S(2)}) collective-permute-start(f32[8,6,16,128]{3,2,1,0:T(8,128)S(1)} %get-tuple-element.27), channel_id=1, source_target_pairs={{0,24},{16,40},{24,0},{32,56},{40,16},{48,72},{56,32},{64,88},{72,... | collective-permute-start | bytes 1179656 | tf_op jit(solution)/shard_map/ppermute | solution.py:224
  45.1 0.1 fusion
  45.2 0.7 collective-permute-done.4
  45.9 0.1 fusion.8
  46.0 2.2 %collective-permute-done.6 = f32[8,6,16,128]{3,2,1,0:T(8,128)S(1)} collective-permute-done((f32[8,6,16,128]{3,2,1,0:T(8,128)S(1)}, f32[8,6,16,128]{3,2,1,0:T(8,128)S(1)}, u32[]{:S(2)}, u32[]{:S(2)}) %collective-permute-start.6) | collective-permute-done | bytes 393248 | tf_op jit(solution)/shard_map/ppermute | solution.py:224
  48.2 6.1 %collective-permute-done.7 = f32[8,6,16,128]{3,2,1,0:T(8,128)S(1)} collective-permute-done((f32[8,6,16,128]{3,2,1,0:T(8,128)S(1)}, f32[8,6,16,128]{3,2,1,0:T(8,128)S(1)}, u32[]{:S(2)}, u32[]{:S(2)}) %collective-permute-start.7) | collective-permute-done | bytes 393248 | tf_op jit(solution)/shard_map/ppermute | solution.py:224
  54.4 0.1 pad_maximum_fusion.2
  54.5 32.5 %all_to_all.10 = f32[8,6,32,128]{3,2,1,0:T(8,128)S(1)} all-to-all(f32[8,6,32,128]{3,2,1,0:T(8,128)S(1)} %pad_maximum_fusion.2), channel_id=1, replica_groups=mesh['dom'=64,'mem'=8] {'mem'}, dimensions={0} | all-to-all | bytes 1572864 | tf_op jit(solution)/shard_map/all_to_all | solution.py:274
  87.0 0.6 shard_map.66
  87.6 12.0 %all_to_all.11 = f32[8,32,128]{2,1,0:T(8,128)S(1)} all-to-all(f32[8,32,128]{2,1,0:T(8,128)S(1)} %shard_map.66), channel_id=1, replica_groups=mesh['dom'=64,'mem'=8] {'mem'}, dimensions={0} | all-to-all | bytes 262144 | tf_op jit(solution)/shard_map/all_to_all | solution.py:280
  99.6 0.7 copy_bitcast_fusion
  (9 shorter events, 0.2 us)
Async XLA Ops:
  4.5 9.3 %collective-permute-start.1 = (f32[2,8,6,32,128]{4,3,2,1,0:T(8,128)S(1)}, f32[2,8,6,32,128]{4,3,2,1,0:T(8,128)S(1)}, u32[]{:S(2)}, u32[]{:S(2)}) collective-permute-start(f32[2,8,6,32,128]{4,3,2,1,0:T(8,128)S(1)} %get-tuple-element.20), channel_id=1, source_target_pairs={{0,8},{8,0},{16,24},{24,16},{32,40},{40,32},{48,56},{56,48},{64,72... | collective-permute-start | bytes 4718600 | tf_op jit(solution)/shard_map/ppermute | solution.py:213
  11.9 15.3 %collective-permute-start = (f32[3,8,6,32,128]{4,3,2,1,0:T(8,128)S(1)}, f32[3,8,6,32,128]{4,3,2,1,0:T(8,128)S(1)}, u32[]{:S(2)}, u32[]{:S(2)}) collective-permute-start(f32[3,8,6,32,128]{4,3,2,1,0:T(8,128)S(1)} %get-tuple-element.18), channel_id=1, source_target_pairs={{0,8},{8,0},{16,24},{24,16},{32,40},{40,32},{48,56},{56,48},{64,72... | collective-permute-start | bytes 7077896 | tf_op jit(solution)/shard_map/ppermute | solution.py:213
  14.1 13.0 %collective-permute-start.2 = (f32[2,8,6,16,128]{4,3,2,1,0:T(8,128)S(1)}, f32[2,8,6,16,128]{4,3,2,1,0:T(8,128)S(1)}, u32[]{:S(2)}, u32[]{:S(2)}) collective-permute-start(f32[2,8,6,16,128]{4,3,2,1,0:T(8,128)S(1)} %pad_maximum_fusion), channel_id=1, source_target_pairs={{0,16},{16,32},{24,8},{32,48},{40,24},{48,64},{56,40},{64,80},{72,... | collective-permute-start | bytes 2359304 | tf_op jit(solution)/shard_map/ppermute | solution.py:224
  16.1 20.5 %collective-permute-start.5 = (f32[2,8,6,16,128]{4,3,2,1,0:T(8,128)S(1)}, f32[2,8,6,16,128]{4,3,2,1,0:T(8,128)S(1)}, u32[]{:S(2)}, u32[]{:S(2)}) collective-permute-start(f32[2,8,6,16,128]{4,3,2,1,0:T(8,128)S(1)} %pad_maximum_fusion.1), channel_id=1, source_target_pairs={{0,16},{16,32},{24,8},{32,48},{40,24},{48,64},{56,40},{64,80},{72,... | collective-permute-start | bytes 2359304 | tf_op jit(solution)/shard_map/ppermute | solution.py:224
  27.4 17.8 %collective-permute-start.3 = (f32[8,6,16,128]{3,2,1,0:T(8,128)S(1)}, f32[8,6,16,128]{3,2,1,0:T(8,128)S(1)}, u32[]{:S(2)}, u32[]{:S(2)}) collective-permute-start(f32[8,6,16,128]{3,2,1,0:T(8,128)S(1)} %get-tuple-element.26), channel_id=1, source_target_pairs={{0,16},{16,32},{24,8},{32,48},{40,24},{48,64},{56,40},{64,80},{72,... | collective-permute-start | bytes 1179656 | tf_op jit(solution)/shard_map/ppermute | solution.py:224
  30.2 15.6 %collective-permute-start.4 = (f32[8,6,16,128]{3,2,1,0:T(8,128)S(1)}, f32[8,6,16,128]{3,2,1,0:T(8,128)S(1)}, u32[]{:S(2)}, u32[]{:S(2)}) collective-permute-start(f32[8,6,16,128]{3,2,1,0:T(8,128)S(1)} %get-tuple-element.25), channel_id=1, source_target_pairs={{0,24},{16,40},{24,0},{32,56},{40,16},{48,72},{56,32},{64,88},{72,... | collective-permute-start | bytes 1179656 | tf_op jit(solution)/shard_map/ppermute | solution.py:224
  36.9 11.3 %collective-permute-start.6 = (f32[8,6,16,128]{3,2,1,0:T(8,128)S(1)}, f32[8,6,16,128]{3,2,1,0:T(8,128)S(1)}, u32[]{:S(2)}, u32[]{:S(2)}) collective-permute-start(f32[8,6,16,128]{3,2,1,0:T(8,128)S(1)} %get-tuple-element.28), channel_id=1, source_target_pairs={{0,16},{16,32},{24,8},{32,48},{40,24},{48,64},{56,40},{64,80},{72,... | collective-permute-start | bytes 1179656 | tf_op jit(solution)/shard_map/ppermute | solution.py:224
  38.8 15.5 %collective-permute-start.7 = (f32[8,6,16,128]{3,2,1,0:T(8,128)S(1)}, f32[8,6,16,128]{3,2,1,0:T(8,128)S(1)}, u32[]{:S(2)}, u32[]{:S(2)}) collective-permute-start(f32[8,6,16,128]{3,2,1,0:T(8,128)S(1)} %get-tuple-element.27), channel_id=1, source_target_pairs={{0,24},{16,40},{24,0},{32,56},{40,16},{48,72},{56,32},{64,88},{72,... | collective-permute-start | bytes 1179656 | tf_op jit(solution)/shard_map/ppermute | solution.py:224
  54.4 32.6 %copy-start = (f32[32,1024]{1,0:T(8,128)S(1)}, f32[32,1024]{1,0:T(8,128)}, u32[]{:S(2)}) copy-start(f32[32,1024]{1,0:T(8,128)} %observed_ref.1) | copy-start | bytes 393220

commit v5 on v4

--- a/solution.py
+++ b/solution.py
@@ -11,7 +11,7 @@
 CHUNKS = (16, 16)
 MIXES = ((0, 1),)
 
-FAR = {4: 0, -3: 1, -4: 2}
+FAR = {4: 0, -3: 2, -4: 3}
 NEAR = {2: 0, 3: 1, 0: 2, -1: 3, -2: 4, 1: 5}
 UNROLL = 4
 
@@ -228,13 +228,13 @@
     groups, _, _ = ensemble.shape
     tiles = (ensemble, tile_weight, tile_block, tile_target, tile_count)
     tiles = tuple(pltpu.with_memory_space_constraint(value, pltpu.HBM) for value in tiles[:4]) + tiles[4:]
-    keep, give, *held = remap(FAR, (1, 2), True, *tiles)
+    keep, give, *held = remap(FAR, (2, 2), True, *tiles)
     from_core = swapped(give)
     ahead = []
     first = 0
     for length in CHUNKS:
         part = slice(first, first + length)
-        value = jnp.concatenate([from_core[:1, :, :, part] + keep[:, :, :, part], from_core[1:, :, :, part]])
+        value = from_core[:, :, :, part] + keep[:, :, :, part]
         ahead.append(passed_on(value, False))
         first += length
     keep, own, give = remap(NEAR, (2, 1, 3), False, *held, *tiles[2:])

time: 101 us -> 103 us (1.020)
  the two profiles are of different devices: /device:TPU:35 before, /device:TPU:56 now
where the time goes in v5:
time: 103 us; the launch traced here: 102 us
  blocking collectives  46.5 us (45%)
  starting transfers between devices  24.8 us (24%)
  waiting for transfers between devices  20.2 us (20%)
  Pallas kernels  8.18 us (8%)
  other arithmetic  1.13 us (1%)
    all_to_all x1, blocking collectives, on_device(): lax.all_to_all(totals[0], 'mem', split_axis=0, concat_axis=0, tiled=True)  34.5 us
    ppermute x6, starting transfers between devices, passed_on(): return lax.ppermute(value, 'dom', pairs)  20.3 us
    ppermute x6, waiting for transfers between devices, passed_on(): return lax.ppermute(value, 'dom', pairs)  20.2 us
    all_to_all x1, blocking collectives, on_device(): lax.all_to_all(copies, 'mem', split_axis=0, concat_axis=0, tiled=True)  12 us
    pallas_call x2, Pallas kernels, remap(): pl.pallas_call(functools.partial(remap_kernel, coded(table), parts, load)...  7.57 us
    ppermute x2, starting transfers between devices, swapped(): lax.ppermute(value, 'dom', [(source, source ^ 1) for source in range(coun...  4.54 us
  transfers between devices with their start and end apart: 8, of which 5 were waited for; matrix products, arithmetic and copies ran while one was open for 1% of the time, Pallas kernels for 5%

profile of v5, /device:TPU:56, one launch (start us, length us, event | category | flops | bytes accessed | tf_op | source)
XLA Modules:
  0.0 102.3 jit_solution(6927752739342039371)
XLA Ops:
  0.7 2.8 %shard_map.64 = (f32[2,8,6,32,128]{4,3,2,1,0:T(8,128)S(1)}, f32[2,8,6,32,128]{4,3,2,1,0:T(8,128)S(1)}, bf16[6,32,4096]{2,1,0:T(8,128)(2,1)S(1)}, bf16[96,128,128]{2,1,0:T(8,128)(2,1)S(1)}) custom-call(s32[96]{0:T(128)} %block_hbm.3, s32[96]{0:T(128)} %target_hbm.3, s32[1]{0:T(128)S(6)} %copy.10.count_hbm, bf16[6,32,4096]{2,1,0:T(8,128)(2,1)} %ens_in.1, ...), custom_call_target="tpu_custom_call" | custom-call | flops 603979776 | bytes 12000000 | tf_op jit(solution)/shard_map/pallas_call | solution.py:123
  3.5 2.4 %collective-permute-start.1 = (f32[2,8,6,32,128]{4,3,2,1,0:T(8,128)S(1)}, f32[2,8,6,32,128]{4,3,2,1,0:T(8,128)S(1)}, u32[]{:S(2)}, u32[]{:S(2)}) collective-permute-start(f32[2,8,6,32,128]{4,3,2,1,0:T(8,128)S(1)} %get-tuple-element.20), channel_id=1, source_target_pairs={{0,8},{8,0},{16,24},{24,16},{32,40},{40,32},{48,56},{56,48},{64,72... | collective-permute-start | bytes 4718600 | tf_op jit(solution)/shard_map/ppermute | solution.py:213
  5.9 4.8 %shard_map.65 = (f32[2,8,6,32,128]{4,3,2,1,0:T(8,128)S(1)}, f32[1,8,6,32,128]{4,3,2,1,0:T(8,128)S(1)}, f32[3,8,6,32,128]{4,3,2,1,0:T(8,128)S(1)}) custom-call(s32[96]{0:T(128)} %block_hbm.3, s32[96]{0:T(128)} %target_hbm.3, s32[1]{0:T(128)S(6)} %copy.10.count_hbm, bf16[6,32,4096]{2,1,0:T(8,128)(2,1)S(1)} %get-tuple-element.15.ens_in, ...), custom_call_target="tpu_custom_call" | custom-call | flops 603979776 | bytes 12000000 | tf_op jit(solution)/shard_map/pallas_call | solution.py:123
  10.6 2.2 %collective-permute-start = (f32[3,8,6,32,128]{4,3,2,1,0:T(8,128)S(1)}, f32[3,8,6,32,128]{4,3,2,1,0:T(8,128)S(1)}, u32[]{:S(2)}, u32[]{:S(2)}) collective-permute-start(f32[3,8,6,32,128]{4,3,2,1,0:T(8,128)S(1)} %get-tuple-element.18), channel_id=1, source_target_pairs={{0,8},{8,0},{16,24},{24,16},{32,40},{40,32},{48,56},{56,48},{64,72... | collective-permute-start | bytes 7077896 | tf_op jit(solution)/shard_map/ppermute | solution.py:213
  12.8 0.2 slice_add_fusion.1
  13.0 2.8 %collective-permute-start.2 = (f32[2,8,6,16,128]{4,3,2,1,0:T(8,128)S(1)}, f32[2,8,6,16,128]{4,3,2,1,0:T(8,128)S(1)}, u32[]{:S(2)}, u32[]{:S(2)}) collective-permute-start(f32[2,8,6,16,128]{4,3,2,1,0:T(8,128)S(1)} %get-tuple-element.29), channel_id=1, source_target_pairs={{0,16},{16,32},{24,8},{32,48},{40,24},{48,64},{56,40},{64,80},{72,... | collective-permute-start | bytes 2359304 | tf_op jit(solution)/shard_map/ppermute | solution.py:224
  15.8 3.3 %collective-permute-start.5 = (f32[2,8,6,16,128]{4,3,2,1,0:T(8,128)S(1)}, f32[2,8,6,16,128]{4,3,2,1,0:T(8,128)S(1)}, u32[]{:S(2)}, u32[]{:S(2)}) collective-permute-start(f32[2,8,6,16,128]{4,3,2,1,0:T(8,128)S(1)} %get-tuple-element.30), channel_id=1, source_target_pairs={{0,16},{16,32},{24,8},{32,48},{40,24},{48,64},{56,40},{64,80},{72,... | collective-permute-start | bytes 2359304 | tf_op jit(solution)/shard_map/ppermute | solution.py:224
  19.1 8.4 %collective-permute-done.2 = f32[2,8,6,16,128]{4,3,2,1,0:T(8,128)S(1)} collective-permute-done((f32[2,8,6,16,128]{4,3,2,1,0:T(8,128)S(1)}, f32[2,8,6,16,128]{4,3,2,1,0:T(8,128)S(1)}, u32[]{:S(2)}, u32[]{:S(2)}) %collective-permute-start.2) | collective-permute-done | bytes 786464 | tf_op jit(solution)/shard_map/ppermute | solution.py:224
  27.5 0.2 fusion.6
  27.8 4.3 %collective-permute-start.3 = (f32[8,6,16,128]{3,2,1,0:T(8,128)S(1)}, f32[8,6,16,128]{3,2,1,0:T(8,128)S(1)}, u32[]{:S(2)}, u32[]{:S(2)}) collective-permute-start(f32[8,6,16,128]{3,2,1,0:T(8,128)S(1)} %get-tuple-element.26), channel_id=1, source_target_pairs={{0,16},{16,32},{24,8},{32,48},{40,24},{48,64},{56,40},{64,80},{72,... | collective-permute-start | bytes 1179656 | tf_op jit(solution)/shard_map/ppermute | solution.py:224
  32.1 3.9 %collective-permute-done.5 = f32[2,8,6,16,128]{4,3,2,1,0:T(8,128)S(1)} collective-permute-done((f32[2,8,6,16,128]{4,3,2,1,0:T(8,128)S(1)}, f32[2,8,6,16,128]{4,3,2,1,0:T(8,128)S(1)}, u32[]{:S(2)}, u32[]{:S(2)}) %collective-permute-start.5) | collective-permute-done | bytes 786464 | tf_op jit(solution)/shard_map/ppermute | solution.py:224
  36.0 1.9 %collective-permute-start.4 = (f32[8,6,16,128]{3,2,1,0:T(8,128)S(1)}, f32[8,6,16,128]{3,2,1,0:T(8,128)S(1)}, u32[]{:S(2)}, u32[]{:S(2)}) collective-permute-start(f32[8,6,16,128]{3,2,1,0:T(8,128)S(1)} %get-tuple-element.25), channel_id=1, source_target_pairs={{0,24},{16,40},{24,0},{32,56},{40,16},{48,72},{56,32},{64,88},{72,... | collective-permute-start | bytes 1179656 | tf_op jit(solution)/shard_map/ppermute | solution.py:224
  37.9 0.2 fusion.2
  38.1 5.7 %collective-permute-start.7 = (f32[8,6,16,128]{3,2,1,0:T(8,128)S(1)}, f32[8,6,16,128]{3,2,1,0:T(8,128)S(1)}, u32[]{:S(2)}, u32[]{:S(2)}) collective-permute-start(f32[8,6,16,128]{3,2,1,0:T(8,128)S(1)} %get-tuple-element.27), channel_id=1, source_target_pairs={{0,24},{16,40},{24,0},{32,56},{40,16},{48,72},{56,32},{64,88},{72,... | collective-permute-start | bytes 1179656 | tf_op jit(solution)/shard_map/ppermute | solution.py:224
  43.9 2.2 %collective-permute-start.6 = (f32[8,6,16,128]{3,2,1,0:T(8,128)S(1)}, f32[8,6,16,128]{3,2,1,0:T(8,128)S(1)}, u32[]{:S(2)}, u32[]{:S(2)}) collective-permute-start(f32[8,6,16,128]{3,2,1,0:T(8,128)S(1)} %get-tuple-element.28), channel_id=1, source_target_pairs={{0,16},{16,32},{24,8},{32,48},{40,24},{48,64},{56,40},{64,80},{72,... | collective-permute-start | bytes 1179656 | tf_op jit(solution)/shard_map/ppermute | solution.py:224
  46.1 0.1 fusion
  46.2 0.9 collective-permute-done.4
  47.2 4.1 %collective-permute-done.7 = f32[8,6,16,128]{3,2,1,0:T(8,128)S(1)} collective-permute-done((f32[8,6,16,128]{3,2,1,0:T(8,128)S(1)}, f32[8,6,16,128]{3,2,1,0:T(8,128)S(1)}, u32[]{:S(2)}, u32[]{:S(2)}) %collective-permute-start.7) | collective-permute-done | bytes 393248 | tf_op jit(solution)/shard_map/ppermute | solution.py:224
  51.4 2.9 %collective-permute-done.6 = f32[8,6,16,128]{3,2,1,0:T(8,128)S(1)} collective-permute-done((f32[8,6,16,128]{3,2,1,0:T(8,128)S(1)}, f32[8,6,16,128]{3,2,1,0:T(8,128)S(1)}, u32[]{:S(2)}, u32[]{:S(2)}) %collective-permute-start.6) | collective-permute-done | bytes 393248 | tf_op jit(solution)/shard_map/ppermute | solution.py:224
  54.3 0.1 pad_maximum_fusion
  54.5 34.5 %all_to_all.10 = f32[8,6,32,128]{3,2,1,0:T(8,128)S(1)} all-to-all(f32[8,6,32,128]{3,2,1,0:T(8,128)S(1)} %pad_maximum_fusion), channel_id=1, replica_groups=mesh['dom'=64,'mem'=8] {'mem'}, dimensions={0} | all-to-all | bytes 1572864 | tf_op jit(solution)/shard_map/all_to_all | solution.py:274
  89.0 0.6 shard_map.66
  89.6 12.0 %all_to_all.11 = f32[8,32,128]{2,1,0:T(8,128)S(1)} all-to-all(f32[8,32,128]{2,1,0:T(8,128)S(1)} %shard_map.66), channel_id=1, replica_groups=mesh['dom'=64,'mem'=8] {'mem'}, dimensions={0} | all-to-all | bytes 262144 | tf_op jit(solution)/shard_map/all_to_all | solution.py:280
  101.6 0.7 copy_bitcast_fusion
  (7 shorter events, 0.2 us)
Async XLA Ops:
  3.5 9.3 %collective-permute-start.1 = (f32[2,8,6,32,128]{4,3,2,1,0:T(8,128)S(1)}, f32[2,8,6,32,128]{4,3,2,1,0:T(8,128)S(1)}, u32[]{:S(2)}, u32[]{:S(2)}) collective-permute-start(f32[2,8,6,32,128]{4,3,2,1,0:T(8,128)S(1)} %get-tuple-element.20), channel_id=1, source_target_pairs={{0,8},{8,0},{16,24},{24,16},{32,40},{40,32},{48,56},{56,48},{64,72... | collective-permute-start | bytes 4718600 | tf_op jit(solution)/shard_map/ppermute | solution.py:213
  10.6 16.9 %collective-permute-start = (f32[3,8,6,32,128]{4,3,2,1,0:T(8,128)S(1)}, f32[3,8,6,32,128]{4,3,2,1,0:T(8,128)S(1)}, u32[]{:S(2)}, u32[]{:S(2)}) collective-permute-start(f32[3,8,6,32,128]{4,3,2,1,0:T(8,128)S(1)} %get-tuple-element.18), channel_id=1, source_target_pairs={{0,8},{8,0},{16,24},{24,16},{32,40},{40,32},{48,56},{56,48},{64,72... | collective-permute-start | bytes 7077896 | tf_op jit(solution)/shard_map/ppermute | solution.py:213
  13.0 14.5 %collective-permute-start.2 = (f32[2,8,6,16,128]{4,3,2,1,0:T(8,128)S(1)}, f32[2,8,6,16,128]{4,3,2,1,0:T(8,128)S(1)}, u32[]{:S(2)}, u32[]{:S(2)}) collective-permute-start(f32[2,8,6,16,128]{4,3,2,1,0:T(8,128)S(1)} %get-tuple-element.29), channel_id=1, source_target_pairs={{0,16},{16,32},{24,8},{32,48},{40,24},{48,64},{56,40},{64,80},{72,... | collective-permute-start | bytes 2359304 | tf_op jit(solution)/shard_map/ppermute | solution.py:224
  15.8 20.1 %collective-permute-start.5 = (f32[2,8,6,16,128]{4,3,2,1,0:T(8,128)S(1)}, f32[2,8,6,16,128]{4,3,2,1,0:T(8,128)S(1)}, u32[]{:S(2)}, u32[]{:S(2)}) collective-permute-start(f32[2,8,6,16,128]{4,3,2,1,0:T(8,128)S(1)} %get-tuple-element.30), channel_id=1, source_target_pairs={{0,16},{16,32},{24,8},{32,48},{40,24},{48,64},{56,40},{64,80},{72,... | collective-permute-start | bytes 2359304 | tf_op jit(solution)/shard_map/ppermute | solution.py:224
  27.8 19.4 %collective-permute-start.3 = (f32[8,6,16,128]{3,2,1,0:T(8,128)S(1)}, f32[8,6,16,128]{3,2,1,0:T(8,128)S(1)}, u32[]{:S(2)}, u32[]{:S(2)}) collective-permute-start(f32[8,6,16,128]{3,2,1,0:T(8,128)S(1)} %get-tuple-element.26), channel_id=1, source_target_pairs={{0,16},{16,32},{24,8},{32,48},{40,24},{48,64},{56,40},{64,80},{72,... | collective-permute-start | bytes 1179656 | tf_op jit(solution)/shard_map/ppermute | solution.py:224
  36.0 11.2 %collective-permute-start.4 = (f32[8,6,16,128]{3,2,1,0:T(8,128)S(1)}, f32[8,6,16,128]{3,2,1,0:T(8,128)S(1)}, u32[]{:S(2)}, u32[]{:S(2)}) collective-permute-start(f32[8,6,16,128]{3,2,1,0:T(8,128)S(1)} %get-tuple-element.25), channel_id=1, source_target_pairs={{0,24},{16,40},{24,0},{32,56},{40,16},{48,72},{56,32},{64,88},{72,... | collective-permute-start | bytes 1179656 | tf_op jit(solution)/shard_map/ppermute | solution.py:224
  38.1 13.2 %collective-permute-start.7 = (f32[8,6,16,128]{3,2,1,0:T(8,128)S(1)}, f32[8,6,16,128]{3,2,1,0:T(8,128)S(1)}, u32[]{:S(2)}, u32[]{:S(2)}) collective-permute-start(f32[8,6,16,128]{3,2,1,0:T(8,128)S(1)} %get-tuple-element.27), channel_id=1, source_target_pairs={{0,24},{16,40},{24,0},{32,56},{40,16},{48,72},{56,32},{64,88},{72,... | collective-permute-start | bytes 1179656 | tf_op jit(solution)/shard_map/ppermute | solution.py:224
  43.9 10.4 %collective-permute-start.6 = (f32[8,6,16,128]{3,2,1,0:T(8,128)S(1)}, f32[8,6,16,128]{3,2,1,0:T(8,128)S(1)}, u32[]{:S(2)}, u32[]{:S(2)}) collective-permute-start(f32[8,6,16,128]{3,2,1,0:T(8,128)S(1)} %get-tuple-element.28), channel_id=1, source_target_pairs={{0,16},{16,32},{24,8},{32,48},{40,24},{48,64},{56,40},{64,80},{72,... | collective-permute-start | bytes 1179656 | tf_op jit(solution)/shard_map/ppermute | solution.py:224
  54.3 34.7 %copy-start = (f32[32,1024]{1,0:T(8,128)S(1)}, f32[32,1024]{1,0:T(8,128)}, u32[]{:S(2)}) copy-start(f32[32,1024]{1,0:T(8,128)} %observed_ref.1) | copy-start | bytes 393220
